TPU v7x, 32 devices: a whole 2x2x4 slice. The times are simulated.
32 devices in a mesh: fsdp: 4 (over z), ctx: 4 (over x, core), tp: 2 (over y).
Axes of the slice: x: 2, y: 2, z: 4, core: 2. Of those that a mesh axis runs over, the one named last changes fastest.
Arguments:
- layer_in: bfloat16 [4, 1024, 1024], P('fsdp', 'ctx'), may hold values from -6 to 6
- segment_ids: int32 [4, 1024], P('fsdp', 'ctx'), may hold values from 0 to 18, as said below
- valid_mask: int32 [4, 1024], P('fsdp', 'ctx'), may hold values from 0 to 1, as said below
- teacher: bfloat16 [4, 1024, 1024], P('fsdp', 'ctx'), may hold values from -6 to 6
- attn_gain: bfloat16 [1024], P('fsdp'), may hold values from 0.099609375 to 1.8984375
- w_query: bfloat16 [1024, 256], P('fsdp', 'tp'), may hold values from -0.1875 to 0.1875
- w_key: bfloat16 [1024, 256], P('fsdp', 'tp'), may hold values from -0.1875 to 0.1875
- w_value: bfloat16 [1024, 1024], P('fsdp', 'tp'), may hold values from -0.1875 to 0.1875
- w_out: bfloat16 [1024, 1024], P('tp', 'fsdp'), may hold values from -2 to 2
- ffn_gain: bfloat16 [1024], P('fsdp'), may hold values from 0.099609375 to 1.8984375
- w_gate: bfloat16 [1024, 2752], P('fsdp', 'tp'), may hold values from -0.1875 to 0.1875
- w_up: bfloat16 [1024, 2752], P('fsdp', 'tp'), may hold values from -0.1875 to 0.1875
- w_down: bfloat16 [2752, 1024], P('tp', 'fsdp'), may hold values from -0.109375 to 0.109375
Outputs:
- layer_out: bfloat16 [4, 1024, 1024], P('fsdp', 'ctx')
- grad_in: bfloat16 [4, 1024, 1024], P('fsdp', 'ctx')
- grad_attn_gain: float32 [1024], P('fsdp')
- grad_query: float32 [1024, 256], P('fsdp', 'tp')
- grad_key: float32 [1024, 256], P('fsdp', 'tp')
- grad_value: float32 [1024, 1024], P('fsdp', 'tp')
- grad_out: float32 [1024, 1024], P('tp', 'fsdp')
- grad_ffn_gain: float32 [1024], P('fsdp')
- grad_gate: float32 [1024, 2752], P('fsdp', 'tp')
- grad_up: float32 [1024, 2752], P('fsdp', 'tp')
- grad_down: float32 [2752, 1024], P('tp', 'fsdp')
- loss_value: float32 [], replicated
Inputs may be any that keep to these rules, and one draw needn't show every extreme that they name: `segment_ids`: within each sequence the ids of valid tokens start at 0 and rise by 0 or 1 from one token to the next; equal ids in a sequence mark one document. Padding tokens carry the largest id, which no document has. `valid_mask`: in each sequence the valid tokens come first; the padding tokens after them, where there are any.
All inputs are finite; a program needn't handle non-finite values.
Results may differ from a plain program's by a relative error of at most 0.014.
Values may be sent and summed in bfloat16 or wider, within the bound.
A program may use at most 128 MiB of HBM per device.

v0:
```python
from functools import partial
import math

import jax
import jax.numpy as jnp
from jax import lax
from jax.sharding import PartitionSpec as P

FEAT = 16
HEAD_V = 64


EPSILON = 1e-05
HIGH = lax.Precision.HIGHEST
QUAD_SCALE = 1.0 / (4.0 * math.sqrt(2.0))


def entering(x, axis, join, neutral):
    place = lax.axis_index(axis)
    gathered = jax.tree.map(
        lambda a, kind: lax.all_gather(a.astype(kind), axis),
        x,
        (jnp.bfloat16, jnp.bfloat16, jnp.bfloat16),
    )
    state = jax.tree.map(lambda a, e: jnp.zeros_like(a) + jnp.asarray(e, a.dtype), x, neutral)

    def one(lap, state):
        return join(
            state,
            jax.tree.map(
                lambda a, own: lax.dynamic_index_in_dim(a, lap, 0, False).astype(own.dtype),
                gathered,
                x,
            ),
        )

    return lax.fori_loop(0, place, one, state)


def entering_2(x, axis, combine, identity):
    devices, here = (lax.axis_size(axis), lax.axis_index(axis))
    everything = jax.tree.map(
        lambda part, kind: lax.all_gather(part.astype(kind), axis),
        x,
        jax.tree.map(lambda a: jnp.bfloat16 if a.dtype == jnp.float32 else a.dtype, x),
    )
    start = jax.tree.map(
        lambda part, zero: jnp.broadcast_to(jnp.asarray(zero, part.dtype), part.shape), x, identity
    )

    def lap(k, before):
        at = devices - 1 - k
        reached = at > here
        new = combine(
            before, jax.tree.map(lambda part, own: part[at].astype(own.dtype), everything, x)
        )
        return jax.tree.map(lambda a, b: jnp.where(reached, a, b), new, before)

    return lax.fori_loop(0, devices, lap, start)


def product(left_side, right_side):
    return jnp.dot(left_side, right_side, preferred_element_type=jnp.float32)


def product_left_t(left_side, right_side):
    return lax.dot_general(
        left_side, right_side, (((0,), (0,)), ((), ())), preferred_element_type=jnp.float32
    )


def product_right_t(left_side, right_side):
    return lax.dot_general(
        left_side, right_side, (((1,), (1,)), ((), ())), preferred_element_type=jnp.float32
    )


def features(vectors):
    lead_dims = vectors.shape[:-1]
    feat_width = vectors.shape[-1]
    square = (vectors[..., :, None] * vectors[..., None, :]).reshape(
        lead_dims + (feat_width * feat_width,)
    )
    return jnp.concatenate(
        [jnp.ones(lead_dims + (1,), jnp.float32), 0.5 * vectors, QUAD_SCALE * square], axis=-1
    )


def attend(query_rows, key_rows, value_rows, prev_state, prev_norm, segment, prev_id):
    scores = jnp.einsum("slhf,smhf->shlm", query_rows, key_rows, precision=HIGH) * 0.25
    kernel = 1.0 + scores + 0.5 * scores * scores
    places = jnp.arange(segment.shape[1])
    allowed = (places[:, None] >= places[None, :])[None] & (
        segment[:, :, None] == segment[:, None, :]
    )
    kernel = jnp.where(allowed[:, None], kernel, 0.0)
    carried = (segment.astype(jnp.float32) == prev_id[:, None]).astype(jnp.float32)
    mapped = features(query_rows) * carried[:, :, None, None]
    numerator = jnp.einsum("shlm,smhv->slhv", kernel, value_rows, precision=HIGH) + jnp.einsum(
        "slht,shtv->slhv", mapped, prev_state, precision=HIGH
    )
    denominator = jnp.einsum("shlm->slh", kernel) + jnp.einsum(
        "slht,sht->slh", mapped, prev_norm, precision=HIGH
    )
    return numerator / denominator[..., None]


def summarize(key_rows, value_rows, segment):
    closing = (segment == segment[:, -1:]).astype(jnp.float32)
    mapped = features(key_rows) * closing[:, :, None, None]
    return (
        jnp.einsum("slht,slhv->shtv", mapped, value_rows, precision=HIGH),
        jnp.sum(mapped, axis=1),
    )


def rms_forward(values_in, gain_vec):
    inv_root = lax.rsqrt(jnp.mean(values_in * values_in, axis=-1, keepdims=True) + EPSILON)
    return (values_in * inv_root * gain_vec, inv_root)


def rms_backward(values_in, inv_root, gain_vec, grad_normed):
    weighted = grad_normed * gain_vec
    grad_gain = jnp.sum(grad_normed * values_in * inv_root, axis=0)
    grad_values = inv_root * weighted - values_in * inv_root**3 * jnp.mean(
        weighted * values_in, axis=-1, keepdims=True
    )
    return (grad_values, grad_gain)


def chain_combine(earlier, later):
    is_fresh = later[0] < 0
    same_doc = later[0] == earlier[0]

    def pick(early_part, late_part):
        expand = (-1,) + (1,) * (early_part.ndim - 1)
        with_early = late_part + jnp.where(same_doc.reshape(expand), early_part, 0.0)
        return jnp.where(is_fresh.reshape(expand), early_part, with_early)

    return (
        jnp.where(is_fresh, earlier[0], later[0]),
        pick(earlier[1], later[1]),
        pick(earlier[2], later[2]),
    )


def tp_forward(partial_sum):
    return lax.psum(partial_sum, "tp")


def tp_backward(partial_sum):
    return lax.psum(partial_sum.astype(jnp.bfloat16), "tp").astype(jnp.float32)


def per_device(
    layer_in,
    segment_ids,
    valid_mask,
    teacher,
    attn_gain,
    w_query,
    w_key,
    w_value,
    w_out,
    ffn_gain,
    w_gate,
    w_up,
    w_down,
):
    full_weights = (
        lax.all_gather(attn_gain, "fsdp", axis=0, tiled=True),
        lax.all_gather(w_query, "fsdp", axis=0, tiled=True),
        lax.all_gather(w_key, "fsdp", axis=0, tiled=True),
        lax.all_gather(w_value, "fsdp", axis=0, tiled=True),
        lax.all_gather(w_out, "fsdp", axis=1, tiled=True),
        lax.all_gather(ffn_gain, "fsdp", axis=0, tiled=True),
        lax.all_gather(w_gate, "fsdp", axis=0, tiled=True),
        lax.all_gather(w_up, "fsdp", axis=0, tiled=True),
        lax.all_gather(w_down, "fsdp", axis=1, tiled=True),
    )
    (
        gain_one,
        full_query,
        full_key,
        full_value,
        full_out,
        gain_two,
        full_gate,
        full_up,
        full_down,
    ) = full_weights
    seq_count, shard_len, model_width = layer_in.shape
    row_count = seq_count * shard_len
    heads_here = full_query.shape[1] // FEAT
    rows_in = layer_in.reshape(row_count, model_width).astype(jnp.float32)
    normed_full, root_one = rms_forward(rows_in, gain_one.astype(jnp.float32))
    normed_one = normed_full.astype(jnp.bfloat16)
    query_rows = product(normed_one, full_query).reshape(seq_count, shard_len, heads_here, FEAT)
    key_rows = product(normed_one, full_key).reshape(seq_count, shard_len, heads_here, FEAT)
    value_rows = product(normed_one, full_value).reshape(seq_count, shard_len, heads_here, HEAD_V)
    last_id = segment_ids[:, -1].astype(jnp.float32)
    first_id = segment_ids[:, 0].astype(jnp.float32)
    (out_state, out_norm), summary_pull = jax.vjp(
        partial(summarize, segment=segment_ids), key_rows, value_rows
    )
    blank_state = jnp.zeros_like(out_state)
    blank_norm = jnp.zeros_like(out_norm)
    no_doc = jnp.full_like(last_id, -1.0)
    prev_id, prev_state, prev_norm = entering(
        (last_id, out_state, out_norm), "ctx", chain_combine, (no_doc, blank_state, blank_norm)
    )
    attended, attend_pull = jax.vjp(
        partial(attend, segment=segment_ids, prev_id=prev_id),
        query_rows,
        key_rows,
        value_rows,
        prev_state,
        prev_norm,
    )
    mixed_heads = attended.reshape(row_count, heads_here * HEAD_V).astype(jnp.bfloat16)
    head_sum = product(mixed_heads, full_out)
    teacher_rows = teacher.reshape(row_count, model_width).astype(jnp.float32)
    weight_rows = valid_mask.reshape(row_count, 1).astype(jnp.float32)
    middle = rows_in + tp_forward(head_sum)
    normed_mid, root_two = rms_forward(middle, gain_two.astype(jnp.float32))
    normed_two = normed_mid.astype(jnp.bfloat16)
    gate_rows = product(normed_two, full_gate)
    up_rows = product(normed_two, full_up)
    sigmoid_gate = jax.nn.sigmoid(gate_rows)
    silu_gate = gate_rows * sigmoid_gate
    hidden = (silu_gate * up_rows).astype(jnp.bfloat16)
    down_sum = product(hidden, full_down)
    output = middle + tp_forward(down_sum)
    misfit = (output - teacher_rows) * weight_rows
    layer_rows = output.astype(jnp.bfloat16)
    grad_rows = misfit.astype(jnp.bfloat16)
    sum_squares = jnp.sum(misfit * misfit)
    sum_valid = jnp.sum(weight_rows)
    back_weights = (
        lax.all_gather(attn_gain, "fsdp", axis=0, tiled=True),
        lax.all_gather(w_query, "fsdp", axis=0, tiled=True),
        lax.all_gather(w_key, "fsdp", axis=0, tiled=True),
        lax.all_gather(w_value, "fsdp", axis=0, tiled=True),
        lax.all_gather(w_out, "fsdp", axis=1, tiled=True),
        lax.all_gather(ffn_gain, "fsdp", axis=0, tiled=True),
        lax.all_gather(w_gate, "fsdp", axis=0, tiled=True),
        lax.all_gather(w_up, "fsdp", axis=0, tiled=True),
        lax.all_gather(w_down, "fsdp", axis=1, tiled=True),
    )
    (
        gain_one,
        full_query,
        full_key,
        full_value,
        full_out,
        gain_two,
        full_gate,
        full_up,
        full_down,
    ) = back_weights
    grad_down = product_left_t(hidden, grad_rows)
    grad_hidden = product_right_t(grad_rows, full_down)
    grad_gate_rows = (
        grad_hidden * up_rows * sigmoid_gate * (1.0 + gate_rows * (1.0 - sigmoid_gate))
    ).astype(jnp.bfloat16)
    grad_up_rows = (grad_hidden * silu_gate).astype(jnp.bfloat16)
    grad_gate = product_left_t(normed_two, grad_gate_rows)
    grad_up = product_left_t(normed_two, grad_up_rows)
    normed_two_terms = product_right_t(grad_gate_rows, full_gate) + product_right_t(
        grad_up_rows, full_up
    )
    grad_normed_two = tp_backward(normed_two_terms)
    grad_mid_norm, grad_ffn_gain = rms_backward(
        middle, root_two, gain_two.astype(jnp.float32), grad_normed_two
    )
    grad_middle = misfit + grad_mid_norm
    grad_branch = grad_middle.astype(jnp.bfloat16)
    grad_out = product_left_t(mixed_heads, grad_branch)
    grad_mixed = product_right_t(grad_branch, full_out).reshape(
        seq_count, shard_len, heads_here, HEAD_V
    )
    grad_q_near, grad_k_near, grad_v_near, grad_prev_state, grad_prev_norm = attend_pull(grad_mixed)
    next_id, later_state, later_norm = entering_2(
        (first_id, grad_prev_state, grad_prev_norm),
        "ctx",
        chain_combine,
        (no_doc, blank_state, blank_norm),
    )
    continues = (next_id == last_id).astype(jnp.float32)
    grad_k_far, grad_v_far = summary_pull(
        (later_state * continues[:, None, None, None], later_norm * continues[:, None, None])
    )
    grad_query_rows = grad_q_near.reshape(row_count, heads_here * FEAT).astype(jnp.bfloat16)
    grad_key_rows = (
        (grad_k_near + grad_k_far).reshape(row_count, heads_here * FEAT).astype(jnp.bfloat16)
    )
    grad_value_rows = (
        (grad_v_near + grad_v_far).reshape(row_count, heads_here * HEAD_V).astype(jnp.bfloat16)
    )
    grad_query = product_left_t(normed_one, grad_query_rows)
    grad_key = product_left_t(normed_one, grad_key_rows)
    grad_value = product_left_t(normed_one, grad_value_rows)
    normed_one_terms = (
        product_right_t(grad_query_rows, full_query)
        + product_right_t(grad_key_rows, full_key)
        + product_right_t(grad_value_rows, full_value)
    )
    grad_normed_one = tp_backward(normed_one_terms)
    grad_rows_in, grad_attn_gain = rms_backward(
        rows_in, root_one, gain_one.astype(jnp.float32), grad_normed_one
    )
    grad_in_rows = (grad_middle + grad_rows_in).astype(jnp.bfloat16)
    total_sq, total_valid = lax.psum((sum_squares, sum_valid), ("fsdp", "ctx"))
    loss_value = total_sq / (total_valid * model_width)
    grad_in = grad_in_rows.reshape(seq_count, shard_len, model_width)
    layer_out = layer_rows.reshape(seq_count, shard_len, model_width)
    owned = (
        lax.psum_scatter(
            grad_attn_gain.astype(jnp.bfloat16), "fsdp", scatter_dimension=0, tiled=True
        ).astype(jnp.float32),
        lax.psum_scatter(
            grad_query.astype(jnp.bfloat16), "fsdp", scatter_dimension=0, tiled=True
        ).astype(jnp.float32),
        lax.psum_scatter(
            grad_key.astype(jnp.bfloat16), "fsdp", scatter_dimension=0, tiled=True
        ).astype(jnp.float32),
        lax.psum_scatter(
            grad_value.astype(jnp.bfloat16), "fsdp", scatter_dimension=0, tiled=True
        ).astype(jnp.float32),
        lax.psum_scatter(
            grad_out.astype(jnp.bfloat16), "fsdp", scatter_dimension=1, tiled=True
        ).astype(jnp.float32),
        lax.psum_scatter(
            grad_ffn_gain.astype(jnp.bfloat16), "fsdp", scatter_dimension=0, tiled=True
        ).astype(jnp.float32),
        lax.psum_scatter(
            grad_gate.astype(jnp.bfloat16), "fsdp", scatter_dimension=0, tiled=True
        ).astype(jnp.float32),
        lax.psum_scatter(
            grad_up.astype(jnp.bfloat16), "fsdp", scatter_dimension=0, tiled=True
        ).astype(jnp.float32),
        lax.psum_scatter(
            grad_down.astype(jnp.bfloat16), "fsdp", scatter_dimension=1, tiled=True
        ).astype(jnp.float32),
    )
    shares = (
        lax.psum(owned[0].astype(jnp.bfloat16), "ctx").astype(jnp.float32),
        lax.psum(owned[1].astype(jnp.bfloat16), "ctx").astype(jnp.float32),
        lax.psum(owned[2].astype(jnp.bfloat16), "ctx").astype(jnp.float32),
        lax.psum(owned[3].astype(jnp.bfloat16), "ctx").astype(jnp.float32),
        lax.psum(owned[4].astype(jnp.bfloat16), "ctx").astype(jnp.float32),
        lax.psum(owned[5].astype(jnp.bfloat16), "ctx").astype(jnp.float32),
        lax.psum(owned[6].astype(jnp.bfloat16), "ctx").astype(jnp.float32),
        lax.psum(owned[7].astype(jnp.bfloat16), "ctx").astype(jnp.float32),
        lax.psum(owned[8].astype(jnp.bfloat16), "ctx").astype(jnp.float32),
    )
    return (
        layer_out,
        grad_in,
        shares[0],
        shares[1],
        shares[2],
        shares[3],
        shares[4],
        shares[5],
        shares[6],
        shares[7],
        shares[8],
        loss_value,
    )


def solution(mesh):
    placed = (
        P("fsdp", "ctx", None),
        P("fsdp", "ctx"),
        P("fsdp", "ctx"),
        P("fsdp", "ctx", None),
        P("fsdp"),
        P("fsdp", "tp"),
        P("fsdp", "tp"),
        P("fsdp", "tp"),
        P("tp", "fsdp"),
        P("fsdp"),
        P("fsdp", "tp"),
        P("fsdp", "tp"),
        P("tp", "fsdp"),
    )
    return jax.shard_map(
        per_device,
        mesh=mesh,
        in_specs=placed,
        out_specs=(
            P("fsdp", "ctx", None),
            P("fsdp", "ctx", None),
            P("fsdp"),
            P("fsdp", "tp"),
            P("fsdp", "tp"),
            P("fsdp", "tp"),
            P("tp", "fsdp"),
            P("fsdp"),
            P("fsdp", "tp"),
            P("fsdp", "tp"),
            P("tp", "fsdp"),
            P(),
        ),
        check_vma=False,
    )
```

profile of v0, /device:TPU:0, one launch (start us, length us, event | category | flops | bytes accessed | tf_op | source)
XLA Modules:
  0.0 834.6 jit_solution(4206275548353771715)
XLA Ops:
  8.6 12.6 %all-gather.5 = bf16[4,1,256]{2,1,0:T(2,128)(2,1)S(1)} all-gather(bf16[1,1,256]{2,1,0:T(2,128)(2,1)S(1)} %reshape.818), channel_id=1, replica_groups=mesh['fsdp'=4,'ctx'=4,'tp'=2] {'fsdp'}, dimensions={0}, use_global_device_ids=true | all-gather | bytes 2560 | tf_op jit(solution)/shard_map/all_gather | solution.py:171
  21.3 16.3 %all_gather.71 = bf16[1024,128]{1,0:T(8,128)(2,1)S(1)} all-gather(bf16[256,128]{1,0:T(8,128)(2,1)} %param.23), channel_id=1, replica_groups=mesh['fsdp'=4,'ctx'=4,'tp'=2] {'fsdp'}, dimensions={0}, use_global_device_ids=true | all-gather | bytes 327680 | tf_op jit(solution)/shard_map/all_gather | solution.py:173
  55.8 5.2 all-gather.2
  62.2 14.5 %all_gather.70 = bf16[1024,128]{1,0:T(8,128)(2,1)S(1)} all-gather(bf16[256,128]{1,0:T(8,128)(2,1)S(1)} %copy-done.48), channel_id=1, replica_groups=mesh['fsdp'=4,'ctx'=4,'tp'=2] {'fsdp'}, dimensions={0}, use_global_device_ids=true | all-gather | bytes 327680 | tf_op jit(solution)/shard_map/all_gather | solution.py:172
  85.4 6.5 all-reduce.6
  107.5 10.1 %all-gather.6 = bf16[4,1,256]{2,1,0:T(2,128)(2,1)S(1)} all-gather(bf16[1,1,256]{2,1,0:T(2,128)(2,1)S(1)} %reshape.820), channel_id=1, replica_groups=mesh['fsdp'=4,'ctx'=4,'tp'=2] {'fsdp'}, dimensions={0}, use_global_device_ids=true | all-gather | bytes 2560 | tf_op jit(solution)/shard_map/all_gather | solution.py:176
  117.7 38.3 %all-reduce.15.cloned.1.call-done = f32[256,1024]{1,0:T(8,128)} async-done(((f32[256,1024]{1,0:T(8,128)}), f32[256,1024]{1,0:T(8,128)}) %all-reduce.15.cloned.1.call-update) | async-done | bytes 1048592 | tf_op jit(solution)/shard_map/psum | solution.py:148
  157.6 57.8 %all-gather.19.cloned.1.call-done = bf16[1024,1376]{0,1:T(8,128)(2,1)} async-done(((bf16[256,1376]{0,1:T(8,128)(2,1)}), bf16[1024,1376]{0,1:T(8,128)(2,1)}) %all-gather.19.cloned.1.call-update) | async-done | bytes 2818064 | tf_op jit(solution)/shard_map/all_gather | solution.py:177
  215.4 3.8 fusion.113
  219.2 53.9 %all-gather.21.cloned.1.call-done = bf16[1024,1376]{0,1:T(8,128)(2,1)} async-done(((bf16[256,1376]{0,1:T(8,128)(2,1)}), bf16[1024,1376]{0,1:T(8,128)(2,1)}) %all-gather.21.cloned.1.call-update) | async-done | bytes 2818064 | tf_op jit(solution)/shard_map/all_gather | solution.py:178
  273.1 4.6 multiply_convert_fusion.2
  277.7 53.2 %all-gather.23.cloned.1.call-done = bf16[1376,1024]{1,0:T(8,128)(2,1)} async-done(((bf16[1376,256]{1,0:T(8,128)(2,1)}), bf16[1376,1024]{1,0:T(8,128)(2,1)}) %all-gather.23.cloned.1.call-update) | async-done | bytes 2818064 | tf_op jit(solution)/shard_map/all_gather | solution.py:179
  330.9 4.0 fusion.114
  335.0 38.4 %all-reduce.17.cloned.1.call-done = f32[256,1024]{1,0:T(8,128)} async-done(((f32[256,1024]{1,0:T(8,128)}), f32[256,1024]{1,0:T(8,128)}) %all-reduce.17.cloned.1.call-update) | async-done | bytes 1048592 | tf_op jit(solution)/shard_map/psum | solution.py:148
  376.5 3.6 multiply_convert_fusion
  384.3 10.9 %all-gather.27.cloned.1.call-start = ((), (), s32[]{:S(2)}) async-start(), calls=%async_computation.24 | async-start | bytes 1966080 | tf_op jit(solution)/shard_map/all_gather | solution.py:43
  395.2 17.9 %all-reduce.19.cloned.1.call-done = bf16[256,1024]{1,0:T(8,128)(2,1)} async-done(((bf16[256,1024]{1,0:T(8,128)(2,1)}), bf16[256,1024]{1,0:T(8,128)(2,1)}) %all-reduce.19.cloned.1.call-update) | async-done | bytes 524304 | tf_op jit(solution)/shard_map/psum | solution.py:152
  422.6 3.8 fusion.89
  426.3 5.2 all-gather.4
  443.5 4.8 fusion.58
  451.4 18.1 %while.35 = (s32[]{:T(128)}, f32[1]{0:T(128)}, f32[1,8,273,64]{3,2,1,0:T(8,128)S(1)}, f32[1,8,273]{2,1,0:T(8,128)S(1)}, s32[]{:T(128)}, /*index=5*/bf16[4,1]{0,1...) while((s32[]{:T(128)}, f32[1]{0:T(128)}, ...), condition=%wide.region_14.15_spmd.clone, body=%wide.region_13.14_spmd.clone.sunk | while | flops 851772 | bytes 2538059 | solution.py:59
  477.6 4.3 fusion.24
  497.7 4.3 reduce-scatter.14.cloned.1.call-done
  501.9 21.3 %reduce-scatter.10.cloned.1.call-done = bf16[256,128]{1,0:T(8,128)(2,1)} async-done(((bf16[1024,128]{1,0:T(8,128)(2,1)}), bf16[256,128]{1,0:T(8,128)(2,1)}) %reduce-scatter.10.cloned.1.call-update) | async-done | bytes 65552 | tf_op jit(solution)/shard_map/reduce_scatter | solution.py:324
  523.3 28.3 %reduce-scatter.12.cloned.1.call-done = bf16[256,512]{1,0:T(8,128)(2,1)} async-done(((bf16[1024,512]{1,0:T(8,128)(2,1)}), bf16[256,512]{1,0:T(8,128)(2,1)}) %reduce-scatter.12.cloned.1.call-update) | async-done | bytes 262160 | tf_op jit(solution)/shard_map/reduce_scatter | solution.py:327
  551.6 56.0 %reduce-scatter.20.cloned.1.call-done = bf16[1376,256]{1,0:T(8,128)(2,1)} async-done(((bf16[1376,1024]{1,0:T(8,128)(2,1)}), bf16[1376,256]{1,0:T(8,128)(2,1)}) %reduce-scatter.20.cloned.1.call-update) | async-done | bytes 704528 | tf_op jit(solution)/shard_map/reduce_scatter | solution.py:342
  607.5 57.2 %reduce-scatter.16.cloned.1.call-done = bf16[256,1376]{0,1:T(8,128)(2,1)} async-done(((bf16[1024,1376]{0,1:T(8,128)(2,1)}), bf16[256,1376]{0,1:T(8,128)(2,1)}) %reduce-scatter.16.cloned.1.call-update) | async-done | bytes 704528 | tf_op jit(solution)/shard_map/reduce_scatter | solution.py:336
  664.7 57.2 %reduce-scatter.18.cloned.1.call-done = bf16[256,1376]{0,1:T(8,128)(2,1)} async-done(((bf16[1024,1376]{0,1:T(8,128)(2,1)}), bf16[256,1376]{0,1:T(8,128)(2,1)}) %reduce-scatter.18.cloned.1.call-update) | async-done | bytes 704528 | tf_op jit(solution)/shard_map/reduce_scatter | solution.py:339
  723.8 32.4 %all-reduce.4 = (f32[]{:T(128)}, f32[]{:T(128)}) all-reduce(f32[]{:T(128)} %get-tuple-element.377, f32[]{:T(128)} %convert_reduce_fusion), channel_id=1, replica_groups=mesh['fsdp'=4,'ctx'=4,'tp'=2] {'fsdp','ctx'}, use_global_device_ids=true, to_apply=%region_40.41 | all-reduce | flops 2 | bytes 16 | tf_op jit(solution)/shard_map/psum | solution.py:313
  758.9 8.4 %all-reduce.8 = (bf16[1024]{0:T(1024)(128)(2,1)S(1)}, bf16[1024]{0:T(1024)(128)(2,1)S(1)}) all-reduce(bf16[1024]{0:T(1024)(128)(2,1)S(1)} %get-tuple-element.328, bf16[1024]{0:T(1024)(128)(2,1)S(1)} %copy-done.55), channel_id=7, replica_groups=mesh['fsdp'=4,'ctx'=4,'tp'=2] {'fsdp'}, use_global_device_ids=true, to_apply=%region_20.21.clone | all-reduce | flops 2048 | bytes 8192
  767.5 6.3 all-reduce.5
  777.1 41.5 %all-reduce.23.cloned.1.call-done = (bf16[256,128]{1,0:T(8,128)(2,1)}, bf16[256,128]{1,0:T(8,128)(2,1)}, bf16[256,512]{1,0:T(8,128)(2,1)}, bf16[512,256]{1,0:T(8...) async-done(((bf16[256,128]{1,0:T(8,128)(2,1)}, bf16[256,128]{1,0:T(8,128)(2,1)}, bf16[256,512]{1,0:T(8,128)(2,1)}, ...) | async-done | bytes 2768912 | tf_op jit(solution)/shard_map/psum | solution.py:348
  (295 shorter events, 124.4 us)
Async XLA Ops:
  7.2 37.4 %all-gather.15.cloned.1.call-start = ((), (), s32[]{:S(2)}) async-start(), calls=%async_computation.7 | async-start | bytes 1310720 | tf_op jit(solution)/shard_map/all_gather | solution.py:174
  7.9 86.6 %all-gather.25.cloned.1.call-start = ((), (), s32[]{:S(2)}) async-start(), calls=%async_computation.23 | async-start | bytes 1966080 | tf_op jit(solution)/shard_map/all_gather | solution.py:21
  44.6 9.7 %copy-start = (f32[256,8,16,16]{0,3,2,1:T(8,128)}, f32[256,8,16,16]{0,3,2,1:T(8,128)S(1)}, u32[]{:S(2)}) copy-start(f32[256,8,16,16]{0,3,2,1:T(8,128)S(1)} %multiply_multiply_fusion.1) | copy-start | bytes 6291460
  52.8 9.4 %copy-start.48 = (bf16[256,128]{1,0:T(8,128)(2,1)S(1)}, bf16[256,128]{1,0:T(8,128)(2,1)}, u32[]{:S(2)}) copy-start(bf16[256,128]{1,0:T(8,128)(2,1)} %param.22) | copy-start | bytes 196612
  52.8 49.9 %all-gather.17.cloned.1.call-start = ((), (), s32[]{:S(2)}) async-start(), calls=%async_computation.8 | async-start | bytes 1310720 | tf_op jit(solution)/shard_map/all_gather | solution.py:175
  53.6 102.4 %all-reduce.15.cloned.1.call-start = ((), (), s32[]{:S(2)}) async-start(), calls=%async_computation.9 | async-start | bytes 2097152 | tf_op jit(solution)/shard_map/psum | solution.py:148
  80.1 11.8 %copy-start.39 = (f32[256,8,64]{0,2,1:T(8,128)S(1)}, f32[256,8,64]{0,2,1:T(8,128)}, u32[]{:S(2)}) copy-start(f32[256,8,64]{0,2,1:T(8,128)} %copy-done.38) | copy-start | bytes 1572868
  80.2 14.4 %copy-start.51 = (pred[256,256]{0,1:T(8,128)(4,1)}, pred[256,256]{0,1:T(8,128)(4,1)S(1)}, u32[]{:S(2)}) copy-start(pred[256,256]{0,1:T(8,128)(4,1)S(1)} %fusion.81) | copy-start | bytes 196612
  82.5 12.1 %copy-start.66 = (f32[8,256,256]{1,2,0:T(8,128)}, f32[8,256,256]{1,2,0:T(8,128)S(1)}, u32[]{:S(2)}) copy-start(f32[8,256,256]{1,2,0:T(8,128)S(1)} %get-tuple-element.399) | copy-start | bytes 6291460
  95.0 327.6 %copy-start.57 = (f32[1,256]{1,0:T(1,128)}, f32[1,256]{1,0:T(1,128)S(1)}, u32[]{:S(2)}) copy-start(f32[1,256]{1,0:T(1,128)S(1)} %compare_convert_fusion) | copy-start | bytes 3076
  105.5 50.4 %copy-start.4 = (bf16[1,256,1024]{2,1,0:T(8,128)(2,1)S(1)}, bf16[1,256,1024]{2,1,0:T(8,128)(2,1)}, u32[]{:S(2)}) copy-start(bf16[1,256,1024]{2,1,0:T(8,128)(2,1)} %param.17) | copy-start | bytes 1572868
  105.6 109.9 %all-gather.19.cloned.1.call-start = ((), (), s32[]{:S(2)}) async-start(), calls=%async_computation.10 | async-start | bytes 3522560 | tf_op jit(solution)/shard_map/all_gather | solution.py:177
  106.1 167.0 %all-gather.21.cloned.1.call-start = ((), (), s32[]{:S(2)}) async-start(), calls=%async_computation.11 | async-start | bytes 3522560 | tf_op jit(solution)/shard_map/all_gather | solution.py:178
  106.7 224.2 %all-gather.23.cloned.1.call-start = ((), (), s32[]{:S(2)}) async-start(), calls=%async_computation.12 | async-start | bytes 3522560 | tf_op jit(solution)/shard_map/all_gather | solution.py:179
  107.5 265.9 %all-reduce.17.cloned.1.call-start = ((), (), s32[]{:S(2)}) async-start(), calls=%async_computation.13 | async-start | bytes 2097152 | tf_op jit(solution)/shard_map/psum | solution.py:148
  157.6 115.5 %copy-start.10 = (bf16[256,1024]{1,0:T(8,128)(2,1)}, bf16[256,1024]{1,0:T(8,128)(2,1)S(1)}, u32[]{:S(2)}) copy-start(bf16[256,1024]{1,0:T(8,128)(2,1)S(1)} %multiply_convert_fusion.3) | copy-start | bytes 1572868
  335.0 78.1 %all-reduce.19.cloned.1.call-start = ((), (), s32[]{:S(2)}) async-start(), calls=%async_computation.14 | async-start | bytes 1048576 | tf_op jit(solution)/shard_map/psum | solution.py:152
  384.3 67.1 %all-gather.27.cloned.1.call-start = ((), (), s32[]{:S(2)}) async-start(), calls=%async_computation.24 | async-start | bytes 1966080 | tf_op jit(solution)/shard_map/all_gather | solution.py:43
  419.1 16.9 %copy-start.14 = (f32[256,512]{0,1:T(8,128)}, f32[256,512]{0,1:T(8,128)S(1)}, u32[]{:S(2)}) copy-start(f32[256,512]{0,1:T(8,128)S(1)} %fusion.76) | copy-start | bytes 1572868
  431.6 66.1 %reduce-scatter.8.cloned.1.call-start = ((), (), s32[]{:S(2)}) async-start(), calls=%async_computation.16 | async-start | bytes 327680 | tf_op jit(solution)/shard_map/reduce_scatter | solution.py:321
  442.0 60.0 %reduce-scatter.14.cloned.1.call-start = ((), (), s32[]{:S(2)}) async-start(), calls=%async_computation.19 | async-start | bytes 1310720 | tf_op jit(solution)/shard_map/reduce_scatter | solution.py:330
  448.3 75.0 %reduce-scatter.10.cloned.1.call-start = ((), (), s32[]{:S(2)}) async-start(), calls=%async_computation.17 | async-start | bytes 327680 | tf_op jit(solution)/shard_map/reduce_scatter | solution.py:324
  477.5 74.0 %reduce-scatter.12.cloned.1.call-start = ((), (), s32[]{:S(2)}) async-start(), calls=%async_computation.18 | async-start | bytes 1310720 | tf_op jit(solution)/shard_map/reduce_scatter | solution.py:327
  484.2 123.3 %reduce-scatter.20.cloned.1.call-start = ((), (), s32[]{:S(2)}) async-start(), calls=%async_computation.22 | async-start | bytes 3522560 | tf_op jit(solution)/shard_map/reduce_scatter | solution.py:342
  486.7 178.0 %reduce-scatter.16.cloned.1.call-start = ((), (), s32[]{:S(2)}) async-start(), calls=%async_computation.20 | async-start | bytes 3522560 | tf_op jit(solution)/shard_map/reduce_scatter | solution.py:336
  490.5 231.5 %reduce-scatter.18.cloned.1.call-start = ((), (), s32[]{:S(2)}) async-start(), calls=%async_computation.21 | async-start | bytes 3522560 | tf_op jit(solution)/shard_map/reduce_scatter | solution.py:339
  494.1 263.4 %all-reduce.21.cloned.1.call-start = ((), (), s32[]{:S(2)}) async-start(), calls=%async_computation.15 | async-start | bytes 1048576 | tf_op jit(solution)/shard_map/psum | solution.py:152
  497.6 224.4 %copy-start.62 = (u32[32]{0:T(128)S(1)}, u32[32]{0:T(128)}, u32[]{:S(2)}) copy-start(u32[32]{0:T(128)} %constant.137) | copy-start | bytes 388
  497.6 225.6 %copy-start.59 = (s32[1,256]{1,0:T(1,128)S(1)}, s32[1,256]{1,0:T(1,128)}, u32[]{:S(2)}) copy-start(s32[1,256]{1,0:T(1,128)} %param.19) | copy-start | bytes 3076
  497.6 261.4 %copy-start.55 = (bf16[1024]{0:T(1024)(128)(2,1)S(1)}, bf16[1024]{0:T(1024)(128)(2,1)}, u32[]{:S(2)}) copy-start(bf16[1024]{0:T(1024)(128)(2,1)} %get-tuple-element.326) | copy-start | bytes 6148
  497.6 277.4 %copy-start.56 = (f32[256]{0:T(256)S(1)}, f32[256]{0:T(256)}, u32[]{:S(2)}) copy-start(f32[256]{0:T(256)} %get-tuple-element.390) | copy-start | bytes 3076
  497.6 321.0 %all-reduce.23.cloned.1.call-start = ((), (), s32[]{:S(2)}) async-start(), calls=%async_computation.25 | async-start | bytes 5537792 | tf_op jit(solution)/shard_map/psum | solution.py:348
  (58 other events, 149.9 us)
Sparse Core Ops, SparseCore 0:
  9.6 34.3 all-gather.14
  53.0 18.2 all-gather.24
  72.8 29.9 all-gather.16
  105.7 50.2 all-reduce.14
  157.4 58.0 all-gather.18
  216.8 56.2 all-gather.20
  274.7 56.2 all-gather.22
  335.1 38.2 all-reduce.16
  384.4 28.6 all-reduce.18
  431.7 19.6 all-gather.26
  453.6 19.9 reduce-scatter.7
  476.4 25.5 reduce-scatter.13
  504.8 18.4 reduce-scatter.9
  526.0 25.5 reduce-scatter.11
  553.7 53.7 reduce-scatter.19
  609.7 54.9 reduce-scatter.15
  666.9 54.9 reduce-scatter.17
  724.6 28.3 all-reduce.20
  755.9 62.6 all-reduce.22
where the time goes:
time: 844 us; the launch traced here: 835 us
  waiting for transfers between devices  532 us (63%)
  blocking collectives  118 us (14%)
  matrix products  83.8 us (10%)
  other arithmetic  33.4 us (4%)
  local copies, waits for them, and re-layouts  27.4 us (3%)
  between operations  19.7 us (2%)
  starting transfers between devices  12.1 us (1%)
    psum x2, waiting for transfers between devices, tp_forward(): return lax.psum(partial_sum, 'tp')  76.7 us
    all_gather x1, waiting for transfers between devices, per_device(): lax.all_gather(w_gate, 'fsdp', axis=0, tiled=True)  57.8 us
    reduce_scatter x1, waiting for transfers between devices, per_device(): lax.psum_scatter(grad_gate.astype(jnp.bfloat16), 'fsdp', scatter_dimensio...  57.2 us
    reduce_scatter x1, waiting for transfers between devices, per_device(): lax.psum_scatter(grad_up.astype(jnp.bfloat16), 'fsdp', scatter_dimension=...  57.2 us
    reduce_scatter x1, waiting for transfers between devices, per_device(): lax.psum_scatter(grad_down.astype(jnp.bfloat16), 'fsdp', scatter_dimensio...  56 us
    all_gather x1, waiting for transfers between devices, per_device(): lax.all_gather(w_up, 'fsdp', axis=0, tiled=True)  53.9 us
    all_gather x1, waiting for transfers between devices, per_device(): lax.all_gather(w_down, 'fsdp', axis=1, tiled=True)  53.2 us
    psum x1, waiting for transfers between devices, per_device(): lax.psum(owned[1].astype(jnp.bfloat16), 'ctx').astype(jnp.float32)  41.5 us
  transfers between devices with their start and end apart: 19, of which 15 were waited for; matrix products, arithmetic and copies ran while one was open for 11% of the time, Pallas kernels for 0%

commit v1 on v0

--- a/solution.py
+++ b/solution.py
@@ -1,9 +1,12 @@
 from functools import partial
+import functools
 import math
 
 import jax
 import jax.numpy as jnp
 from jax import lax
+from jax.experimental import pallas as pl
+from jax.experimental.pallas import tpu as pltpu
 from jax.sharding import PartitionSpec as P
 
 FEAT = 16
@@ -150,6 +153,156 @@
 
 def tp_backward(partial_sum):
     return lax.psum(partial_sum.astype(jnp.bfloat16), "tp").astype(jnp.float32)
+
+
+MESH = pl.DeviceIdType.MESH
+
+def dev(z=None, c=None, t=None):
+    d={}
+    if z is not None: d["fsdp"]=z
+    if c is not None: d["ctx"]=c
+    if t is not None: d["tp"]=t
+    return d
+
+class Gather:
+    def __init__(self, n, groups, sems):
+        self.n=n; self.groups=groups
+        self.z=lax.axis_index("fsdp"); ctx=lax.axis_index("ctx")
+        self.x=ctx//2; self.c=ctx%2
+        self.ic=self.x*2+(1-self.c); self.xp=(1-self.x)*2+self.c
+        (self.zr,self.xr,self.i1r,self.i2r,self.zsl,self.zsr,self.xs,self.i1s,self.i2s)=sems
+    def q(self,g,s,x,c):
+        ref,kind,lo,sz=self.groups[g]
+        if kind=="row":
+            R=ref.shape[0]//self.n
+            return ref.at[pl.ds(pl.multiple_of(s*R+c*(R//2)+x*(R//4)+lo,16),sz),:]
+        C=ref.shape[1]//self.n; H=ref.shape[0]//2
+        return ref.at[pl.ds(pl.multiple_of(x*H+lo,16),sz), pl.ds(pl.multiple_of(s*C+c*(C//2),C//2),C//2)]
+    def cp(self,g,s,x,c,ss,rs,d):
+        r=self.q(g,s,x,c)
+        return pltpu.make_async_remote_copy(src_ref=r,dst_ref=r,send_sem=ss,recv_sem=rs,device_id=d,device_id_type=MESH)
+    def left(self,g,s): return self.cp(g,s,self.x,self.c,self.zsl.at[g,s],self.zr.at[g,s],dev(z=self.z-1))
+    def right(self,g,s): return self.cp(g,s,self.x,self.c,self.zsr.at[g,s],self.zr.at[g,s],dev(z=self.z+1))
+    def ic1(self,g,s,x,c): return self.cp(g,s,x,c,self.i1s.at[g,s],self.i1r.at[g,s],dev(c=self.ic))
+    def ic2(self,g,s,x,c): return self.cp(g,s,x,c,self.i2s.at[g,s],self.i2r.at[g,s],dev(c=self.ic))
+    def xc(self,g,s,x,c): return self.cp(g,s,x,c,self.xs.at[g,s],self.xr.at[g,s],dev(c=self.xp))
+    def own(self,g):
+        z=self.z
+        @pl.when(z>0)
+        def _(): self.left(g,z).start()
+        @pl.when(z<self.n-1)
+        def _(): self.right(g,z).start()
+    def hop(self,g,h):
+        z,x,c,n=self.z,self.x,self.c,self.n
+        for d in (1,-1):
+            s=z+d*h
+            ok=(s<n) if d==1 else (s>=0)
+            @pl.when(ok)
+            def _():
+                self.cp(g,s,x,c,self.zsl.at[g,s],self.zr.at[g,s],dev(z=z)).wait_recv()
+                if d==1:
+                    @pl.when(z>0)
+                    def _(): self.left(g,s).start()
+                else:
+                    @pl.when(z<n-1)
+                    def _(): self.right(g,s).start()
+                self.xc(g,s,x,c).start()
+                self.ic1(g,s,x,c).start()
+    def hopx(self,g,h):
+        z,x,c,n=self.z,self.x,self.c,self.n
+        for d in (1,-1):
+            s=z+d*h
+            ok=(s<n) if d==1 else (s>=0)
+            @pl.when(ok)
+            def _():
+                self.xc(g,s,1-x,c).wait_recv()
+                self.ic2(g,s,1-x,c).start()
+    def finish(self,g):
+        z,x,c,n=self.z,self.x,self.c,self.n
+        @pl.loop(0,n)
+        def _(s):
+            @pl.when(s!=z)
+            def _():
+                self.ic1(g,s,x,1-c).wait_recv()
+                self.ic2(g,s,1-x,1-c).wait_recv()
+    def drain(self):
+        z,x,c,n=self.z,self.x,self.c,self.n
+        for g in range(len(self.groups)):
+            @pl.loop(0,n)
+            def _(s):
+                @pl.when((s>=z)&(z>0))
+                def _(): self.left(g,s).wait_send()
+                @pl.when((s<=z)&(z<n-1))
+                def _(): self.right(g,s).wait_send()
+                @pl.when(s!=z)
+                def _():
+                    self.xc(g,s,x,c).wait_send()
+                    self.ic1(g,s,x,c).wait_send()
+                    self.ic2(g,s,1-x,c).wait_send()
+
+def barrier(n):
+    z=lax.axis_index("fsdp"); ctx=lax.axis_index("ctx"); t=lax.axis_index("tp")
+    b=pltpu.get_barrier_semaphore()
+    x=ctx//2;c=ctx%2
+    @pl.when(z>0)
+    def _(): pl.semaphore_signal(b,inc=1,device_id=dev(z=z-1),device_id_type=MESH)
+    @pl.when(z<n-1)
+    def _(): pl.semaphore_signal(b,inc=1,device_id=dev(z=z+1),device_id_type=MESH)
+    pl.semaphore_signal(b,inc=1,device_id=dev(c=x*2+1-c),device_id_type=MESH)
+    pl.semaphore_signal(b,inc=1,device_id=dev(c=(1-x)*2+c),device_id_type=MESH)
+    cnt=2+(z>0).astype(jnp.int32)+(z<n-1).astype(jnp.int32)
+    pl.semaphore_wait(b,cnt)
+
+def gkernel(n,*refs):
+    ins=refs[:7]; outs=refs[7:12]; lsem=refs[12]; sems=refs[13:]
+    wq,wk,wv,wo,wg,wu,wd=ins
+    fqkv,fo,fg,fu,fd=outs
+    z=lax.axis_index("fsdp")
+    CFG=(1,1,2,2,2); LA=2; LG=2
+    groups=[]; need=[]
+    def split(tot,k):
+        u=tot//16; e=[(u*i//k)*16 for i in range(k+1)]
+        return [(e[i],e[i+1]-e[i]) for i in range(k)]
+    for ref,kind,k,nd in [(fqkv,"row",(CFG[0]),[0,1,2]),(fo,"col",(CFG[1]),[3]),(fg,"row",(CFG[2]),[4]),(fu,"row",(CFG[3]),[5]),(fd,"col",(CFG[4]),[6])]:
+        tot=ref.shape[0]//n//4 if kind=="row" else ref.shape[0]//2
+        for i,(lo,sz) in enumerate(split(tot,k)):
+            groups.append((ref,kind,lo,sz)); need.append(nd if i==0 else [])
+    G=Gather(n,groups,sems)
+    R=wq.shape[0]; C=wo.shape[1]
+    rows=pl.ds(pl.multiple_of(z*R,R),R); cols=pl.ds(pl.multiple_of(z*C,C),C)
+    qa=wq.shape[1]; ka=qa+wk.shape[1]; va=ka+wv.shape[1]
+    loc=[(wq,fqkv.at[rows,0:qa]),(wk,fqkv.at[rows,qa:ka]),(wv,fqkv.at[rows,ka:va]),(wo,fo.at[:,cols]),(wg,fg.at[rows,:]),(wu,fu.at[rows,:]),(wd,fd.at[:,cols])]
+    cps=[pltpu.make_async_copy(a,b,lsem.at[i]) for i,(a,b) in enumerate(loc)]
+    for c in cps: c.start()
+    barrier(n)
+    ng=len(groups)
+    def own(g):
+        for i in need[g]: cps[i].wait()
+        G.own(g)
+    for g in range(LA): own(g)
+    for k in range(ng+n+LG):
+        if k+LA<ng: own(k+LA)
+        for h in range(1,n):
+            if 0<=k-(h-1)<ng: G.hop(k-(h-1),h)
+        for h in range(1,n):
+            if 0<=k-LG-(h-1)<ng: G.hopx(k-LG-(h-1),h)
+    for g in range(ng): G.finish(g)
+    G.drain()
+
+def gather(n,wq,wk,wv,wo,wg,wu,wd):
+    R=wq.shape[0]; C=wo.shape[1]
+    bf=jnp.bfloat16
+    outs=(jax.ShapeDtypeStruct((n*R,wq.shape[1]+wk.shape[1]+wv.shape[1]),bf),
+      jax.ShapeDtypeStruct((wo.shape[0],n*C),bf),
+      jax.ShapeDtypeStruct((n*R,wg.shape[1]),bf),jax.ShapeDtypeStruct((n*R,wu.shape[1]),bf),
+      jax.ShapeDtypeStruct((wd.shape[0],n*C),bf))
+    D=pltpu.SemaphoreType.DMA
+    return pl.pallas_call(functools.partial(gkernel,n),out_shape=outs,
+      in_specs=[pl.BlockSpec(memory_space=pl.ANY)]*7,
+      out_specs=[pl.BlockSpec(memory_space=pltpu.VMEM)]*5,
+      scratch_shapes=[D((7,))]+[D((24,n)) for _ in range(9)],
+      compiler_params=pltpu.CompilerParams(collective_id=0,has_side_effects=True,vmem_limit_bytes=60*2**20),
+      name="gather_weights")(wq,wk,wv,wo,wg,wu,wd)
 
 
 def per_device(
@@ -167,28 +320,40 @@
     w_up,
     w_down,
 ):
-    full_weights = (
-        lax.all_gather(attn_gain, "fsdp", axis=0, tiled=True),
-        lax.all_gather(w_query, "fsdp", axis=0, tiled=True),
-        lax.all_gather(w_key, "fsdp", axis=0, tiled=True),
-        lax.all_gather(w_value, "fsdp", axis=0, tiled=True),
-        lax.all_gather(w_out, "fsdp", axis=1, tiled=True),
-        lax.all_gather(ffn_gain, "fsdp", axis=0, tiled=True),
-        lax.all_gather(w_gate, "fsdp", axis=0, tiled=True),
-        lax.all_gather(w_up, "fsdp", axis=0, tiled=True),
-        lax.all_gather(w_down, "fsdp", axis=1, tiled=True),
-    )
-    (
-        gain_one,
-        full_query,
-        full_key,
-        full_value,
-        full_out,
-        gain_two,
-        full_gate,
-        full_up,
-        full_down,
-    ) = full_weights
+    n = lax.axis_size("fsdp")
+    ctx = lax.axis_size("ctx")
+    if ctx == 4 and w_gate.shape[0] % 64 == 0 and w_out.shape[1] % 256 == 0:
+        gain_one = lax.all_gather(attn_gain, "fsdp", axis=0, tiled=True)
+        gain_two = lax.all_gather(ffn_gain, "fsdp", axis=0, tiled=True)
+        full_qkv, full_out, full_gate, full_up, full_down = gather(
+            n, w_query, w_key, w_value, w_out, w_gate, w_up, w_down
+        )
+        qa = w_query.shape[1]
+        ka = qa + w_key.shape[1]
+        full_query, full_key, full_value = full_qkv[:, :qa], full_qkv[:, qa:ka], full_qkv[:, ka:]
+    else:
+        full_weights = (
+            lax.all_gather(attn_gain, "fsdp", axis=0, tiled=True),
+            lax.all_gather(w_query, "fsdp", axis=0, tiled=True),
+            lax.all_gather(w_key, "fsdp", axis=0, tiled=True),
+            lax.all_gather(w_value, "fsdp", axis=0, tiled=True),
+            lax.all_gather(w_out, "fsdp", axis=1, tiled=True),
+            lax.all_gather(ffn_gain, "fsdp", axis=0, tiled=True),
+            lax.all_gather(w_gate, "fsdp", axis=0, tiled=True),
+            lax.all_gather(w_up, "fsdp", axis=0, tiled=True),
+            lax.all_gather(w_down, "fsdp", axis=1, tiled=True),
+        )
+        (
+            gain_one,
+            full_query,
+            full_key,
+            full_value,
+            full_out,
+            gain_two,
+            full_gate,
+            full_up,
+            full_down,
+        ) = full_weights
     seq_count, shard_len, model_width = layer_in.shape
     row_count = seq_count * shard_len
     heads_here = full_query.shape[1] // FEAT
@@ -236,28 +401,6 @@
     grad_rows = misfit.astype(jnp.bfloat16)
     sum_squares = jnp.sum(misfit * misfit)
     sum_valid = jnp.sum(weight_rows)
-    back_weights = (
-        lax.all_gather(attn_gain, "fsdp", axis=0, tiled=True),
-        lax.all_gather(w_query, "fsdp", axis=0, tiled=True),
-        lax.all_gather(w_key, "fsdp", axis=0, tiled=True),
-        lax.all_gather(w_value, "fsdp", axis=0, tiled=True),
-        lax.all_gather(w_out, "fsdp", axis=1, tiled=True),
-        lax.all_gather(ffn_gain, "fsdp", axis=0, tiled=True),
-        lax.all_gather(w_gate, "fsdp", axis=0, tiled=True),
-        lax.all_gather(w_up, "fsdp", axis=0, tiled=True),
-        lax.all_gather(w_down, "fsdp", axis=1, tiled=True),
-    )
-    (
-        gain_one,
-        full_query,
-        full_key,
-        full_value,
-        full_out,
-        gain_two,
-        full_gate,
-        full_up,
-        full_down,
-    ) = back_weights
     grad_down = product_left_t(hidden, grad_rows)
     grad_hidden = product_right_t(grad_rows, full_down)
     grad_gate_rows = (

time: 844 us -> 706 us (0.84)
  waiting for transfers between devices: 532 us -> 371 us
  Pallas kernels: 0 us -> 69.1 us
  blocking collectives: 118 us -> 82.8 us
  starting transfers between devices: 12.1 us -> 1.22 us
  local copies, waits for them, and re-layouts: 27.4 us -> 37.8 us
  matrix products: 83.8 us -> 74.7 us
    all_gather x5 -> x0, waiting for transfers between devices: 166 us -> none  [the longest x1 57.8 us: per_device(): lax.all_gather(w_gate, 'fsdp', axis=0, tiled=True)]
    pallas_call x0 -> x1, Pallas kernels: none -> 69.1 us  [gather(): pl.pallas_call(functools.partial(gkernel, n), out_shape=outs, in_specs=[p...]
    all_gather x4 -> x2, blocking collectives: 53.5 us -> 18 us  [the longest x1 10 us: per_device(): gain_one = lax.all_gather(attn_gain, 'fsdp', axis=0, tiled=True)]
    all_gather x1, starting transfers between devices: 10.9 us -> 0.04 us  [entering_2(): lax.all_gather(part.astype(kind), axis)]
    psum x2, waiting for transfers between devices: 17.9 us -> 28.8 us  [tp_backward(): return lax.psum(partial_sum.astype(jnp.bfloat16), 'tp').astype(jnp.float32)]
    dot_general x7, matrix products: 19.4 us -> 10.4 us  [product(): return jnp.dot(left_side, right_side, preferred_element_type=jnp.float32)]
    unnamed x152 -> x156, local copies, waits for them, and re-layouts: 15 us -> 22.5 us
  transfers between devices with their start and end apart: 19 -> 14, of which waited for: 15 -> 9; matrix products, arithmetic and copies ran while one was open for 11% -> 10% of each run, Pallas kernels for 0% -> 0%
where the time goes in v1:
time: 706 us; the launch traced here: 697 us
  waiting for transfers between devices  371 us (53%)
  blocking collectives  82.8 us (12%)
  matrix products  74.7 us (11%)
  Pallas kernels  69.1 us (10%)
  local copies, waits for them, and re-layouts  37.8 us (5%)
  other arithmetic  32.9 us (5%)
  between operations  19.7 us (3%)
  loops' own time  8.07 us (1%)
    psum x2, waiting for transfers between devices, tp_forward(): return lax.psum(partial_sum, 'tp')  82.5 us
    pallas_call x1, Pallas kernels, gather(): pl.pallas_call(functools.partial(gkernel, n), out_shape=outs, in_specs=[p...  69.1 us
    reduce_scatter x1, waiting for transfers between devices, per_device(): lax.psum_scatter(grad_up.astype(jnp.bfloat16), 'fsdp', scatter_dimension=...  57.3 us
    reduce_scatter x1, waiting for transfers between devices, per_device(): lax.psum_scatter(grad_down.astype(jnp.bfloat16), 'fsdp', scatter_dimensio...  57.2 us
    reduce_scatter x1, waiting for transfers between devices, per_device(): lax.psum_scatter(grad_gate.astype(jnp.bfloat16), 'fsdp', scatter_dimensio...  56 us
    psum x1, waiting for transfers between devices, per_device(): lax.psum(owned[1].astype(jnp.bfloat16), 'ctx').astype(jnp.float32)  41.5 us
    psum x1, blocking collectives, per_device(): total_sq, total_valid = lax.psum((sum_squares, sum_valid), ('fsdp', 'ctx'))  32.4 us
    psum x2, waiting for transfers between devices, tp_backward(): return lax.psum(partial_sum.astype(jnp.bfloat16), 'tp').astype(jnp.float32)  28.8 us
  transfers between devices with their start and end apart: 14, of which 9 were waited for; matrix products, arithmetic and copies ran while one was open for 10% of the time, Pallas kernels for 0%

profile of v1, /device:TPU:0, one launch (start us, length us, event | category | flops | bytes accessed | tf_op | source)
XLA Modules:
  0.0 696.8 jit_solution(13221310847679128496)
XLA Ops:
  11.7 69.1 %gather_weights.1 = (bf16[1024,768]{1,0:T(8,128)(2,1)}, bf16[512,1024]{1,0:T(8,128)(2,1)}, bf16[1024,1376]{1,0:T(8,128)(2,1)}, bf16[1024,1376]{1,0:T(8,128)(2,1)}, bf16[1376,1024]{1,0:T(8,128)(2,1)}) custom-call(bf16[256,128]{1,0:T(8,128)(2,1)} %refs_0_.1, bf16[256,128]{1,0:T(8,128)(2,1)} %refs_1_.1, bf16[256,512]{1,0:T(8,128)(2,1)} %refs_2_.1, ...), custom_call_target="tpu_custom_call" | custom-call | tf_op jit(solution)/shard_map/gather_weights/pallas_call | solution.py:300
  84.2 10.0 %all-gather.5 = bf16[4,1,256]{2,1,0:T(2,128)(2,1)S(1)} all-gather(bf16[1,1,256]{2,1,0:T(2,128)(2,1)S(1)} %reshape.818), channel_id=1, replica_groups=mesh['fsdp'=4,'ctx'=4,'tp'=2] {'fsdp'}, dimensions={0}, use_global_device_ids=true | all-gather | bytes 2560 | tf_op jit(solution)/shard_map/all_gather | solution.py:326
  101.5 3.5 fusion.18
  109.7 7.0 %all-reduce.6 = (bf16[4]{0:T(256)(128)(2,1)S(1)}, bf16[4]{0:T(256)(128)(2,1)}) all-reduce(bf16[4]{0:T(256)(128)(2,1)S(1)} %dynamic-update-slice, bf16[4]{0:T(256)(128)(2,1)S(1)} %dynamic-update-slice.1), channel_id=2, replica_groups=mesh['fsdp'=4,'ctx'=4,'tp'=2] {'ctx'}, use_global_device_ids=true, to_apply=%add | all-reduce | flops 8 | bytes 32
  118.2 5.4 all-gather.2
  130.2 2.6 fusion.61
  133.8 3.2 fusion.90
  137.0 3.4 divide_convert_fusion
  142.0 8.0 %all-gather.6 = bf16[4,1,256]{2,1,0:T(2,128)(2,1)S(1)} all-gather(bf16[1,1,256]{2,1,0:T(2,128)(2,1)S(1)} %reshape.820), channel_id=1, replica_groups=mesh['fsdp'=4,'ctx'=4,'tp'=2] {'fsdp'}, dimensions={0}, use_global_device_ids=true | all-gather | bytes 2560 | tf_op jit(solution)/shard_map/all_gather | solution.py:327
  150.0 42.3 %all-reduce.15.cloned.1.call-done = f32[256,1024]{1,0:T(8,128)} async-done(((f32[256,1024]{1,0:T(8,128)}), f32[256,1024]{1,0:T(8,128)}) %all-reduce.15.cloned.1.call-update) | async-done | bytes 1048592 | tf_op jit(solution)/shard_map/psum | solution.py:151
  201.7 40.2 %all-reduce.17.cloned.1.call-done = f32[256,1024]{1,0:T(8,128)} async-done(((f32[256,1024]{1,0:T(8,128)}), f32[256,1024]{1,0:T(8,128)}) %all-reduce.17.cloned.1.call-update) | async-done | bytes 1048592 | tf_op jit(solution)/shard_map/psum | solution.py:151
  241.8 3.1 multiply_reduce_fusion.4
  245.0 3.6 multiply_convert_fusion
  252.8 28.7 %all-reduce.19.cloned.1.call-done = bf16[256,1024]{1,0:T(8,128)(2,1)} async-done(((bf16[256,1024]{1,0:T(8,128)(2,1)}), bf16[256,1024]{1,0:T(8,128)(2,1)}) %all-reduce.19.cloned.1.call-update) | async-done | bytes 524304 | tf_op jit(solution)/shard_map/psum | solution.py:155
  287.6 3.3 fusion.25
  291.3 3.8 fusion.93
  295.1 5.2 all-gather.4
  300.3 2.8 fusion.5
  304.9 2.5 fusion.7
  312.1 4.8 fusion.59
  317.3 18.1 %while.35 = (s32[]{:T(128)}, f32[1]{0:T(128)}, f32[1,8,273,64]{3,2,1,0:T(8,128)S(1)}, f32[1,8,273]{2,1,0:T(8,128)S(1)}, s32[]{:T(128)}, /*index=5*/bf16[4,1]{0,1...) while((s32[]{:T(128)}, f32[1]{0:T(128)}, ...), condition=%wide.region_14.15_spmd.clone, body=%wide.region_13.14_spmd.clone.sunk | while | flops 851772 | bytes 2538075 | solution.py:62
  335.4 3.1 fusion.4
  343.7 4.3 fusion.24
  364.1 18.6 %reduce-scatter.10.cloned.1.call-done = bf16[256,128]{1,0:T(8,128)(2,1)} async-done(((bf16[1024,128]{1,0:T(8,128)(2,1)}), bf16[256,128]{1,0:T(8,128)(2,1)}) %reduce-scatter.10.cloned.1.call-update) | async-done | bytes 65552 | tf_op jit(solution)/shard_map/reduce_scatter | solution.py:467
  382.7 28.4 %reduce-scatter.12.cloned.1.call-done = bf16[256,512]{1,0:T(8,128)(2,1)} async-done(((bf16[1024,512]{1,0:T(8,128)(2,1)}), bf16[256,512]{1,0:T(8,128)(2,1)}) %reduce-scatter.12.cloned.1.call-update) | async-done | bytes 262160 | tf_op jit(solution)/shard_map/reduce_scatter | solution.py:470
  411.2 56.0 %reduce-scatter.16.cloned.1.call-done = bf16[256,1376]{0,1:T(8,128)(2,1)} async-done(((bf16[1024,1376]{0,1:T(8,128)(2,1)}), bf16[256,1376]{0,1:T(8,128)(2,1)}) %reduce-scatter.16.cloned.1.call-update) | async-done | bytes 704528 | tf_op jit(solution)/shard_map/reduce_scatter | solution.py:479
  467.2 57.3 %reduce-scatter.18.cloned.1.call-done = bf16[256,1376]{0,1:T(8,128)(2,1)} async-done(((bf16[1024,1376]{0,1:T(8,128)(2,1)}), bf16[256,1376]{0,1:T(8,128)(2,1)}) %reduce-scatter.18.cloned.1.call-update) | async-done | bytes 704528 | tf_op jit(solution)/shard_map/reduce_scatter | solution.py:482
  524.5 57.2 %reduce-scatter.20.cloned.1.call-done = bf16[1376,256]{1,0:T(8,128)(2,1)} async-done(((bf16[1376,1024]{1,0:T(8,128)(2,1)}), bf16[1376,256]{1,0:T(8,128)(2,1)}) %reduce-scatter.20.cloned.1.call-update) | async-done | bytes 704528 | tf_op jit(solution)/shard_map/reduce_scatter | solution.py:485
  583.6 32.4 %all-reduce.4 = (f32[]{:T(128)}, f32[]{:T(128)}) all-reduce(f32[]{:T(128)} %get-tuple-element.403, f32[]{:T(128)} %convert_reduce_fusion), channel_id=1, replica_groups=mesh['fsdp'=4,'ctx'=4,'tp'=2] {'fsdp','ctx'}, use_global_device_ids=true, to_apply=%region_40.41 | all-reduce | flops 2 | bytes 16 | tf_op jit(solution)/shard_map/psum | solution.py:456
  618.7 8.4 %all-reduce.8 = (bf16[1024]{0:T(1024)(128)(2,1)S(1)}, bf16[1024]{0:T(1024)(128)(2,1)S(1)}) all-reduce(bf16[1024]{0:T(1024)(128)(2,1)S(1)} %get-tuple-element.354, bf16[1024]{0:T(1024)(128)(2,1)S(1)} %copy-done.53), channel_id=7, replica_groups=mesh['fsdp'=4,'ctx'=4,'tp'=2] {'fsdp'}, use_global_device_ids=true, to_apply=%region_20.21.clone | all-reduce | flops 2048 | bytes 8192
  627.2 6.4 all-reduce.5
  636.9 41.5 %all-reduce.23.cloned.1.call-done = (bf16[256,128]{1,0:T(8,128)(2,1)}, bf16[256,128]{1,0:T(8,128)(2,1)}, bf16[256,512]{1,0:T(8,128)(2,1)}, bf16[512,256]{1,0:T(8...) async-done(((bf16[256,128]{1,0:T(8,128)(2,1)}, bf16[256,128]{1,0:T(8,128)(2,1)}, bf16[256,512]{1,0:T(8,128)(2,1)}, ...) | async-done | bytes 2768912 | tf_op jit(solution)/shard_map/psum | solution.py:491
  (285 shorter events, 102.8 us)
Async XLA Ops:
  7.2 125.6 %all-gather.10.cloned.1.call-start = ((), (), s32[]{:S(2)}) async-start(), calls=%async_computation.18 | async-start | bytes 1966080 | tf_op jit(solution)/shard_map/all_gather | solution.py:24
  80.8 13.5 %copy-start.3 = (bf16[1,256,1024]{2,1,0:T(8,128)(2,1)S(1)}, bf16[1,256,1024]{2,1,0:T(8,128)(2,1)}, u32[]{:S(2)}) copy-start(bf16[1,256,1024]{2,1,0:T(8,128)(2,1)} %param.17) | copy-start | bytes 1572868
  95.9 21.7 %copy-start = (f32[256,8,16,16]{0,3,2,1:T(8,128)}, f32[256,8,16,16]{0,3,2,1:T(8,128)S(1)}, u32[]{:S(2)}) copy-start(f32[256,8,16,16]{0,3,2,1:T(8,128)S(1)} %multiply_multiply_fusion.1) | copy-start | bytes 6291460
  96.0 5.5 copy-start.43
  100.7 6.2 copy-start.65
  105.0 87.3 %all-reduce.15.cloned.1.call-start = ((), (), s32[]{:S(2)}) async-start(), calls=%async_computation.7 | async-start | bytes 2097152 | tf_op jit(solution)/shard_map/psum | solution.py:151
  117.6 6.2 copy-start.46
  123.8 5.0 copy-start.49
  133.0 158.3 %copy-start.55 = (f32[1,256]{1,0:T(1,128)}, f32[1,256]{1,0:T(1,128)S(1)}, u32[]{:S(2)}) copy-start(f32[1,256]{1,0:T(1,128)S(1)} %compare_convert_fusion) | copy-start | bytes 3076
  140.4 9.5 %copy-start.35 = (bf16[1,256,8,64]{1,3,2,0:T(8,128)(2,1)}, bf16[1,256,8,64]{1,3,2,0:T(8,128)(2,1)S(1)}, u32[]{:S(2)}) copy-start(bf16[1,256,8,64]{1,3,2,0:T(8,128)(2,1)S(1)} %get-tuple-element.428) | copy-start | bytes 786436
  140.4 51.9 %copy-start.4 = (bf16[1,256,1024]{2,1,0:T(8,128)(2,1)S(1)}, bf16[1,256,1024]{2,1,0:T(8,128)(2,1)}, u32[]{:S(2)}) copy-start(bf16[1,256,1024]{2,1,0:T(8,128)(2,1)} %param.17) | copy-start | bytes 1572868
  141.9 99.9 %all-reduce.17.cloned.1.call-start = ((), (), s32[]{:S(2)}) async-start(), calls=%async_computation.8 | async-start | bytes 2097152 | tf_op jit(solution)/shard_map/psum | solution.py:151
  201.6 80.0 %all-reduce.19.cloned.1.call-start = ((), (), s32[]{:S(2)}) async-start(), calls=%async_computation.9 | async-start | bytes 1048576 | tf_op jit(solution)/shard_map/psum | solution.py:155
  252.8 64.5 %all-gather.12.cloned.1.call-start = ((), (), s32[]{:S(2)}) async-start(), calls=%async_computation.19 | async-start | bytes 1966080 | tf_op jit(solution)/shard_map/all_gather | solution.py:46
  287.6 17.1 %copy-start.15 = (f32[256,512]{0,1:T(8,128)}, f32[256,512]{0,1:T(8,128)S(1)}, u32[]{:S(2)}) copy-start(f32[256,512]{0,1:T(8,128)S(1)} %fusion.77) | copy-start | bytes 1572868
  291.1 73.0 %reduce-scatter.8.cloned.1.call-start = ((), (), s32[]{:S(2)}) async-start(), calls=%async_computation.11 | async-start | bytes 327680 | tf_op jit(solution)/shard_map/reduce_scatter | solution.py:464
  310.6 53.5 %reduce-scatter.14.cloned.1.call-start = ((), (), s32[]{:S(2)}) async-start(), calls=%async_computation.14 | async-start | bytes 1310720 | tf_op jit(solution)/shard_map/reduce_scatter | solution.py:473
  312.1 5.1 copy-start.64
  317.0 65.8 %reduce-scatter.10.cloned.1.call-start = ((), (), s32[]{:S(2)}) async-start(), calls=%async_computation.12 | async-start | bytes 327680 | tf_op jit(solution)/shard_map/reduce_scatter | solution.py:467
  339.5 4.1 copy-start.44
  343.6 67.5 %reduce-scatter.12.cloned.1.call-start = ((), (), s32[]{:S(2)}) async-start(), calls=%async_computation.13 | async-start | bytes 1310720 | tf_op jit(solution)/shard_map/reduce_scatter | solution.py:470
  350.3 116.9 %reduce-scatter.16.cloned.1.call-start = ((), (), s32[]{:S(2)}) async-start(), calls=%async_computation.15 | async-start | bytes 3522560 | tf_op jit(solution)/shard_map/reduce_scatter | solution.py:479
  352.8 171.7 %reduce-scatter.18.cloned.1.call-start = ((), (), s32[]{:S(2)}) async-start(), calls=%async_computation.16 | async-start | bytes 3522560 | tf_op jit(solution)/shard_map/reduce_scatter | solution.py:482
  356.4 225.3 %reduce-scatter.20.cloned.1.call-start = ((), (), s32[]{:S(2)}) async-start(), calls=%async_computation.17 | async-start | bytes 3522560 | tf_op jit(solution)/shard_map/reduce_scatter | solution.py:485
  360.4 256.9 %all-reduce.21.cloned.1.call-start = ((), (), s32[]{:S(2)}) async-start(), calls=%async_computation.10 | async-start | bytes 1048576 | tf_op jit(solution)/shard_map/psum | solution.py:155
  364.0 217.8 %copy-start.63 = (u32[32]{0:T(128)S(1)}, u32[32]{0:T(128)}, u32[]{:S(2)}) copy-start(u32[32]{0:T(128)} %constant.137) | copy-start | bytes 388
  364.0 219.0 %copy-start.57 = (s32[1,256]{1,0:T(1,128)S(1)}, s32[1,256]{1,0:T(1,128)}, u32[]{:S(2)}) copy-start(s32[1,256]{1,0:T(1,128)} %param.19) | copy-start | bytes 3076
  364.0 254.7 %copy-start.53 = (bf16[1024]{0:T(1024)(128)(2,1)S(1)}, bf16[1024]{0:T(1024)(128)(2,1)}, u32[]{:S(2)}) copy-start(bf16[1024]{0:T(1024)(128)(2,1)} %get-tuple-element.352) | copy-start | bytes 6148
  364.0 270.7 %copy-start.54 = (f32[256]{0:T(256)S(1)}, f32[256]{0:T(256)}, u32[]{:S(2)}) copy-start(f32[256]{0:T(256)} %get-tuple-element.418) | copy-start | bytes 3076
  364.0 314.4 %all-reduce.23.cloned.1.call-start = ((), (), s32[]{:S(2)}) async-start(), calls=%async_computation.20 | async-start | bytes 5537792 | tf_op jit(solution)/shard_map/psum | solution.py:491
  678.4 6.7 copy-start.39
  678.4 7.9 %copy-start.38 = (bf16[256,1376]{0,1:T(8,128)(2,1)S(1)}, bf16[256,1376]{0,1:T(8,128)(2,1)}, u32[]{:S(2)}) copy-start(bf16[256,1376]{0,1:T(8,128)(2,1)} %get-tuple-element.399) | copy-start | bytes 2113540
  (54 other events, 116.0 us)
Sparse Core Ops, SparseCore 0:
  105.1 17.0 all-gather.9
  142.0 50.2 all-reduce.14
  201.7 40.0 all-reduce.16
  252.9 28.6 all-reduce.18
  291.2 19.6 all-gather.11
  313.0 19.9 reduce-scatter.7
  335.8 25.5 reduce-scatter.13
  364.2 18.4 reduce-scatter.9
  385.6 25.5 reduce-scatter.11
  413.3 53.7 reduce-scatter.15
  469.5 54.9 reduce-scatter.17
  526.7 54.9 reduce-scatter.19
  584.6 28.2 all-reduce.20
  615.7 62.6 all-reduce.22

commit v2 on v0

--- a/solution.py
+++ b/solution.py
@@ -1,9 +1,12 @@
 from functools import partial
+from types import SimpleNamespace
 import math
 
 import jax
 import jax.numpy as jnp
 from jax import lax
+from jax.experimental import pallas as pl
+from jax.experimental.pallas import tpu as pltpu
 from jax.sharding import PartitionSpec as P
 
 FEAT = 16
@@ -152,7 +155,7 @@
     return lax.psum(partial_sum.astype(jnp.bfloat16), "tp").astype(jnp.float32)
 
 
-def per_device(
+def general(
     layer_in,
     segment_ids,
     valid_mask,
@@ -236,28 +239,6 @@
     grad_rows = misfit.astype(jnp.bfloat16)
     sum_squares = jnp.sum(misfit * misfit)
     sum_valid = jnp.sum(weight_rows)
-    back_weights = (
-        lax.all_gather(attn_gain, "fsdp", axis=0, tiled=True),
-        lax.all_gather(w_query, "fsdp", axis=0, tiled=True),
-        lax.all_gather(w_key, "fsdp", axis=0, tiled=True),
-        lax.all_gather(w_value, "fsdp", axis=0, tiled=True),
-        lax.all_gather(w_out, "fsdp", axis=1, tiled=True),
-        lax.all_gather(ffn_gain, "fsdp", axis=0, tiled=True),
-        lax.all_gather(w_gate, "fsdp", axis=0, tiled=True),
-        lax.all_gather(w_up, "fsdp", axis=0, tiled=True),
-        lax.all_gather(w_down, "fsdp", axis=1, tiled=True),
-    )
-    (
-        gain_one,
-        full_query,
-        full_key,
-        full_value,
-        full_out,
-        gain_two,
-        full_gate,
-        full_up,
-        full_down,
-    ) = back_weights
     grad_down = product_left_t(hidden, grad_rows)
     grad_hidden = product_right_t(grad_rows, full_down)
     grad_gate_rows = (
@@ -370,6 +351,1121 @@
     )
 
 
+MESH = pl.DeviceIdType.MESH
+F32 = jnp.float32
+BF16 = jnp.bfloat16
+
+
+def up_to(size, step):
+    return -(-size // step) * step
+
+
+def mm(a, b):
+    return jnp.dot(a, b, preferred_element_type=F32)
+
+
+def mm_nt(a, b):
+    return lax.dot_general(a, b, (((1,), (1,)), ((), ())), preferred_element_type=F32)
+
+
+def mm_tn(a, b):
+    return lax.dot_general(a, b, (((0,), (0,)), ((), ())), preferred_element_type=F32)
+
+
+def at128(offset):
+    return pl.multiple_of(offset, 128)
+
+
+class Place:
+    def __init__(self, n):
+        self.n = n
+        self.z = lax.axis_index("fsdp")
+        self.b = lax.axis_index("ctx")
+        self.t = lax.axis_index("tp")
+        self.x = self.b // 2
+        self.c = self.b % 2
+        self.ic = self.x * 2 + (1 - self.c)
+        self.xp = (1 - self.x) * 2 + self.c
+        self.dg = (1 - self.x) * 2 + (1 - self.c)
+
+
+def remote(src, dst, send, recv, **where):
+    return pltpu.make_async_remote_copy(
+        src_ref=src, dst_ref=dst, send_sem=send, recv_sem=recv, device_id=where, device_id_type=MESH
+    )
+
+
+def entry_barrier(p):
+    sem = pltpu.get_barrier_semaphore()
+    for s in range(p.n):
+
+        @pl.when(p.z != s)
+        def _():
+            pl.semaphore_signal(sem, inc=1, device_id={"fsdp": s}, device_id_type=MESH)
+
+    for peer in (p.ic, p.xp, p.dg):
+        pl.semaphore_signal(sem, inc=1, device_id={"ctx": peer}, device_id_type=MESH)
+    pl.semaphore_signal(sem, inc=1, device_id={"tp": 1 - p.t}, device_id_type=MESH)
+    pl.semaphore_wait(sem, p.n - 1 + 4)
+
+
+class Gather:
+    def __init__(self, p, pieces, sems):
+        self.p = p
+        self.pieces = pieces
+        (self.zr, self.xr, self.i1r, self.i2r, self.zsl, self.zsr, self.xs, self.i1s, self.i2s) = sems
+
+    def quarter(self, g, s, x, c):
+        ref, kind, lo, size = self.pieces[g]
+        n = self.p.n
+        if kind == "row":
+            return ref.at[pl.ds(pl.multiple_of((c * n + s) * 128 + x * 64 + lo[0], 16), size), 0 : lo[1]]
+        half = lo[1]
+        return ref.at[
+            pl.ds(pl.multiple_of(x * half + lo[0], 16), size), pl.ds(at128((c * n + s) * 128), 128)
+        ]
+
+    def copy(self, g, s, x, c, send, recv, **where):
+        ref = self.quarter(g, s, x, c)
+        return remote(ref, ref, send.at[g, s], recv.at[g, s], **where)
+
+    def left(self, g, s):
+        return self.copy(g, s, self.p.x, self.p.c, self.zsl, self.zr, fsdp=self.p.z - 1)
+
+    def right(self, g, s):
+        return self.copy(g, s, self.p.x, self.p.c, self.zsr, self.zr, fsdp=self.p.z + 1)
+
+    def chip(self, g, s, x, c, second):
+        if second:
+            return self.copy(g, s, x, c, self.i2s, self.i2r, ctx=self.p.ic)
+        return self.copy(g, s, x, c, self.i1s, self.i1r, ctx=self.p.ic)
+
+    def cross(self, g, s, x, c):
+        return self.copy(g, s, x, c, self.xs, self.xr, ctx=self.p.xp)
+
+    def own(self, g):
+        p = self.p
+
+        @pl.when(p.z > 0)
+        def _():
+            self.left(g, p.z).start()
+
+        @pl.when(p.z < p.n - 1)
+        def _():
+            self.right(g, p.z).start()
+
+    def hop(self, g, h):
+        p = self.p
+        for d in (1, -1):
+            s = p.z + d * h
+            there = (s < p.n) if d == 1 else (s >= 0)
+
+            @pl.when(there)
+            def _():
+                self.copy(g, s, p.x, p.c, self.zsl, self.zr, fsdp=p.z).wait_recv()
+                if d == 1:
+
+                    @pl.when(p.z > 0)
+                    def _():
+                        self.left(g, s).start()
+
+                else:
+
+                    @pl.when(p.z < p.n - 1)
+                    def _():
+                        self.right(g, s).start()
+
+                self.cross(g, s, p.x, p.c).start()
+                self.chip(g, s, p.x, p.c, False).start()
+
+    def hop_cross(self, g, h):
+        p = self.p
+        for d in (1, -1):
+            s = p.z + d * h
+            there = (s < p.n) if d == 1 else (s >= 0)
+
+            @pl.when(there)
+            def _():
+                self.cross(g, s, 1 - p.x, p.c).wait_recv()
+                self.chip(g, s, 1 - p.x, p.c, True).start()
+
+    def finish(self, g):
+        p = self.p
+
+        @pl.loop(0, p.n)
+        def _(s):
+            @pl.when(s != p.z)
+            def _():
+                self.chip(g, s, p.x, 1 - p.c, False).wait_recv()
+                self.chip(g, s, 1 - p.x, 1 - p.c, True).wait_recv()
+
+    def drain(self):
+        p = self.p
+        for g in range(len(self.pieces)):
+
+            @pl.loop(0, p.n)
+            def _(s):
+                @pl.when((s >= p.z) & (p.z > 0))
+                def _():
+                    self.left(g, s).wait_send()
+
+                @pl.when((s <= p.z) & (p.z < p.n - 1))
+                def _():
+                    self.right(g, s).wait_send()
+
+                @pl.when(s != p.z)
+                def _():
+                    self.cross(g, s, p.x, p.c).wait_send()
+                    self.chip(g, s, p.x, p.c, False).wait_send()
+                    self.chip(g, s, 1 - p.x, p.c, True).wait_send()
+
+
+class Reduce:
+    def __init__(self, p, parts, seen, done, sems):
+        self.p = p
+        self.parts = parts
+        self.seen = seen
+        self.done = done
+        (self.ss, self.rs, self.fs, self.fr) = sems
+
+    def move(self, g, s, slot, to):
+        return remote(
+            self.parts[g].at[s], self.seen[g].at[slot], self.ss.at[g, s], self.rs.at[g, slot], fsdp=to
+        )
+
+    def arrived(self, g, slot):
+        self.move(g, 0, slot, self.p.z).wait_recv()
+
+    def add(self, g, s, slot):
+        total = self.parts[g][s].astype(F32) + self.seen[g][slot].astype(F32)
+        self.parts[g][s] = total.astype(BF16)
+
+    def stage(self, g, k):
+        p = self.p
+        n = p.n
+
+        @pl.when(p.z == k)
+        def _():
+            for s in range(n - 1, k, -1):
+                if k > 0:
+                    self.arrived(g, s)
+                    self.add(g, s, s)
+                self.move(g, s, s, k + 1).start()
+
+        @pl.when(p.z == n - 1 - k)
+        def _():
+            z = n - 1 - k
+            for s in range(0, z):
+                if k > 0:
+                    self.arrived(g, s)
+                    self.add(g, s, s)
+                self.move(g, s, n if s == z - 1 else s, z - 1).start()
+
+    def last(self, g):
+        p = self.p
+        n = p.n
+
+        @pl.when(p.z > 0)
+        def _():
+            self.arrived(g, p.z)
+            self.add(g, p.z, p.z)
+
+        @pl.when(p.z < n - 1)
+        def _():
+            self.arrived(g, n)
+            self.add(g, p.z, n)
+
+        self.done[g][p.b] = self.parts[g][p.z]
+        self.spread(g, p.b, 0, p.ic).start()
+        self.spread(g, p.b, 1, p.xp).start()
+
+    def spread(self, g, slot, which, to):
+        return remote(
+            self.done[g].at[slot], self.done[g].at[slot], self.fs.at[g, which], self.fr.at[g, slot], ctx=to
+        )
+
+    def relay(self, g):
+        p = self.p
+        self.spread(g, p.xp, 1, p.xp).wait_recv()
+        self.spread(g, p.xp, 2, p.ic).start()
+
+    def finish(self, g):
+        p = self.p
+        self.spread(g, p.ic, 0, p.ic).wait_recv()
+        self.spread(g, p.dg, 2, p.ic).wait_recv()
+        self.spread(g, p.b, 0, p.ic).wait_send()
+        self.spread(g, p.b, 1, p.xp).wait_send()
+        self.spread(g, p.xp, 2, p.ic).wait_send()
+
+        @pl.loop(0, p.n)
+        def _(s):
+            @pl.when(s != p.z)
+            def _():
+                self.move(g, s, 0, p.z).wait_send()
+
+
+class Columns:
+    def __init__(self, p, k, src, dst, sems):
+        self.p = p
+        self.k = k
+        self.src = src
+        self.dst = dst
+        self.send, self.recv = sems
+
+    def slot(self, b):
+        rows = self.src.shape[0]
+        return self.dst.at[pl.ds(pl.multiple_of(b * rows, rows), rows), :]
+
+    def copy(self, peer, which):
+        p = self.p
+        w = self.dst.shape[1]
+        part = self.src.at[:, pl.ds(at128((peer % 2) * w), w)]
+        return remote(part, self.slot(p.b), self.send.at[self.k, which], self.recv.at[self.k, p.b], ctx=peer)
+
+    def start(self):
+        p = self.p
+        w = self.dst.shape[1]
+        for which, peer in enumerate((p.xp, p.dg, p.ic)):
+            self.copy(peer, which).start()
+        self.slot(p.b)[...] = self.src[:, pl.ds(at128(p.c * w), w)]
+
+    def wait(self):
+        p = self.p
+        for peer in (p.ic, p.xp, p.dg):
+            remote(self.slot(peer), self.slot(peer), self.send.at[self.k, 0], self.recv.at[self.k, peer], ctx=peer).wait_recv()
+
+    def drain(self):
+        p = self.p
+        for which, peer in enumerate((p.xp, p.dg, p.ic)):
+            self.copy(peer, which).wait_send()
+
+
+class Halves:
+    def __init__(self, p, k, src, dst, step, sems):
+        self.p = p
+        self.k = k
+        self.src = src
+        self.dst = dst
+        self.step = step
+        self.send, self.recv = sems
+
+    def slot(self, b):
+        rows = self.src.shape[0]
+        return self.dst.at[pl.ds(pl.multiple_of(b * rows, rows), rows), :]
+
+    def part(self, x):
+        return self.src.at[:, pl.ds(at128(x * self.step), self.dst.shape[1])]
+
+    def to(self, src, slot, which, peer):
+        return remote(src, self.slot(slot), self.send.at[self.k, which], self.recv.at[self.k, slot], ctx=peer)
+
+    def start(self):
+        p = self.p
+        self.to(self.part(1 - p.x), p.b, 0, p.xp).start()
+        self.to(self.part(p.x), p.b, 1, p.ic).start()
+        self.slot(p.b)[...] = self.src[:, pl.ds(at128(p.x * self.step), self.dst.shape[1])]
+
+    def relay(self):
+        p = self.p
+        self.to(self.slot(p.xp), p.xp, 2, p.ic).wait_recv()
+        self.to(self.slot(p.xp), p.xp, 2, p.ic).start()
+
+    def wait(self):
+        p = self.p
+        self.to(self.slot(p.ic), p.ic, 1, p.ic).wait_recv()
+        self.to(self.slot(p.dg), p.dg, 1, p.ic).wait_recv()
+
+    def drain(self):
+        p = self.p
+        self.to(self.part(1 - p.x), p.b, 0, p.xp).wait_send()
+        self.to(self.part(p.x), p.b, 1, p.ic).wait_send()
+        self.to(self.slot(p.xp), p.xp, 2, p.ic).wait_send()
+
+
+def mega_kernel(n, names, *refs):
+    r = SimpleNamespace(**dict(zip(names, refs)))
+    p = Place(n)
+    z, b, x, c = p.z, p.b, p.x, p.c
+    rows_here = r.x.shape[0]
+    width = r.x.shape[1]
+    half_d = width // 2
+    heads = r.wv.shape[1] // HEAD_V
+    qk = r.wq.shape[1]
+    vw = r.wv.shape[1]
+    ff = r.wd.shape[0]
+    ffp = r.hid.shape[1]
+    order = [s * 256 + cc * 128 for cc in range(2) for s in range(n)]
+    blocks = width // 256
+    D = r.lsem
+
+    fqkv, fo, fg, fu, fd = r.fqkv, r.fo, r.fg, r.fu, r.fd
+    local = []
+
+    def bring(src, dst):
+        copy = pltpu.make_async_copy(src, dst, D.at[len(local)])
+        copy.start()
+        local.append(copy)
+        return copy
+
+    get_x = bring(r.x, r.xv)
+    need = {}
+    for cc in range(2):
+        rows = pl.ds(at128((cc * n + z) * 128), 128)
+        src = slice(cc * 128, cc * 128 + 128)
+        need.setdefault("qkv", []).extend(
+            (
+                bring(r.wq.at[src, :], fqkv.at[rows, 0:qk]),
+                bring(r.wk.at[src, :], fqkv.at[rows, qk : 2 * qk]),
+                bring(r.wv.at[src, :], fqkv.at[rows, 2 * qk : 2 * qk + vw]),
+            )
+        )
+    for cc in range(2):
+        cols = pl.ds(at128((cc * n + z) * 128), 128)
+        need.setdefault("o", []).append(bring(r.wo.at[:, cc * 128 : cc * 128 + 128], fo.at[:, cols]))
+    for cc in range(2):
+        rows = pl.ds(at128((cc * n + z) * 128), 128)
+        need.setdefault("g", []).append(bring(r.wg.at[cc * 128 : cc * 128 + 128, :], fg.at[rows, :]))
+        need.setdefault("u", []).append(bring(r.wu.at[cc * 128 : cc * 128 + 128, :], fu.at[rows, :]))
+    for cc in range(2):
+        cols = pl.ds(at128((cc * n + z) * 128), 128)
+        need.setdefault("d", []).append(
+            bring(r.wd.at[:, cc * 128 : cc * 128 + 128], fd.at[0:ff, cols])
+        )
+    get_teacher = bring(r.teacher, r.tv)
+
+    pieces, first = [], []
+
+    def split(total, parts):
+        unit = total // 16
+        edge = [(unit * i // parts) * 16 for i in range(parts + 1)]
+        return [(edge[i], edge[i + 1] - edge[i]) for i in range(parts)]
+
+    for key, ref, kind, total, parts in (
+        ("qkv", fqkv, "row", 64, 1),
+        ("o", fo, "col", vw // 2, 1),
+        ("g", fg, "row", 64, 2),
+        ("u", fu, "row", 64, 2),
+        ("d", fd, "col", ff // 2, 2),
+    ):
+        for i, (lo, size) in enumerate(split(total, parts)):
+            pieces.append((ref, kind, (lo, ref.shape[1]) if kind == "row" else (lo, total), size))
+            first.append(need[key] if i == 0 else [])
+    gather = Gather(p, pieces, r.gs)
+    ng = len(pieces)
+
+    def own(g):
+        for copy in first[g]:
+            copy.wait()
+        gather.own(g)
+
+    entry_barrier(p)
+    own(0)
+    own(1)
+
+    gsend, grecv, gath = r.gnsem[0], r.gnsem[1], r.gath
+    for s in range(n):
+
+        @pl.when(z != s)
+        def _():
+            remote(r.gains, gath.at[z], gsend.at[s], grecv.at[z], fsdp=s).start()
+
+    gath[z] = r.gains[...]
+    segs, segr = r.segsem[0], r.segsem[1]
+    for i, peer in enumerate((p.ic, p.xp, p.dg)):
+        remote(r.segrow, r.segall.at[b], segs.at[i], segr.at[b], ctx=peer).start()
+    r.segall[b] = r.segrow[...]
+
+    pad = ffp - ff
+    if pad:
+        fd[ff:ffp, :] = jnp.zeros((pad, width), BF16)
+
+    for s in range(n):
+
+        @pl.when(z != s)
+        def _():
+            remote(r.gains, gath.at[s], gsend.at[s], grecv.at[s], fsdp=s).wait_recv()
+
+    for row in range(2):
+        r.gain[row : row + 1, :] = jnp.concatenate(
+            [gath[s, row : row + 1, cc * 128 : cc * 128 + 128] for cc in range(2) for s in range(n)], axis=1
+        )
+
+    events = [(g - 1.5, "own", g, 0) for g in range(2, ng)]
+    for g in range(ng):
+        for h in range(1, n):
+            events.append((g + 0.7 * h, "hop", g, h))
+            events.append((g + 0.7 * h + 0.8, "cross", g, h))
+    events.sort()
+    passed = [0]
+
+    def advance(until):
+        while passed[0] < len(events) and events[passed[0]][0] <= until:
+            _, kind, g, h = events[passed[0]]
+            if kind == "own":
+                own(g)
+            elif kind == "hop":
+                gather.hop(g, h)
+            else:
+                gather.hop_cross(g, h)
+            passed[0] += 1
+
+    def ready(g_from, g_to):
+        advance(max(e[0] for e in events if e[1] == "cross" and e[2] < g_to))
+        for g in range(g_from, g_to):
+            gather.finish(g)
+
+    send_n1 = Columns(p, 0, r.n1, r.n1c, r.csem)
+    send_da = Columns(p, 1, r.da, r.dac, r.csem)
+    send_n2 = Columns(p, 2, r.n2, r.n2c, r.csem)
+    send_dy = Columns(p, 3, r.dy, r.dyc, r.csem)
+    fh = r.hidx.shape[1]
+    send_hid = Halves(p, 0, r.hid, r.hidx, ffp - fh, r.hsem)
+    send_dg = Halves(p, 1, r.dg, r.dgx, ffp - fh, r.hsem)
+    send_du = Halves(p, 2, r.du, r.dux, ffp - fh, r.hsem)
+    send_mix = Halves(p, 3, r.mix, r.mixx, vw // 2, r.hsem)
+    send_dqkv = Halves(p, 4, r.dqkv, r.dqkvx, (2 * qk + vw) // 2, r.hsem)
+    ysend, yrecv = r.ysend, r.yrecv
+
+    def y_copy(i, ch):
+        return remote(ysend.at[i, ch], yrecv.at[i, ch], r.ysem[0].at[i, ch], r.ysem[1].at[i, ch], tp=1 - p.t)
+
+    def y_put(i, ch, value):
+        ysend[i, ch] = value.astype(BF16)
+        y_copy(i, ch).start()
+
+    def y_wait(i, between=()):
+        for ch in range(blocks):
+            y_copy(i, ch).wait_recv()
+            if ch < len(between):
+                between[ch]()
+
+    def y_rows(i, rs):
+        return jnp.concatenate(
+            [ysend[i, ch, rs, :].astype(F32) + yrecv[i, ch, rs, :].astype(F32) for ch in range(blocks)], axis=1
+        )
+
+    step_rows = 32
+    row_steps = rows_here // step_rows
+
+    def per_rows(body):
+        @pl.loop(0, row_steps)
+        def _(i):
+            body(pl.ds(pl.multiple_of(i * step_rows, step_rows), step_rows))
+
+    def x_rows(rs):
+        return jnp.concatenate([r.xv[rs, o : o + 128] for o in order], axis=1).astype(F32)
+
+    def rsq(v):
+        return lax.rsqrt(jnp.mean(v * v, axis=1, keepdims=True) + EPSILON)
+
+    get_x.wait()
+
+    def norm_one(rs):
+        v = x_rows(rs)
+        r.n1[rs, :] = (v * rsq(v) * r.gain[0:1, :]).astype(BF16)
+
+    per_rows(norm_one)
+    ready(0, 1)
+    kv = r.kv
+    first_chunk = mm(r.n1[...], fqkv[:, 0 : 2 * qk])
+    r.q[...] = first_chunk[:, 0:qk].astype(BF16)
+    kv[b, :, 0:qk] = first_chunk[:, qk : 2 * qk].astype(BF16)
+    for ch in range(vw // 256):
+        lo = ch * 256
+        kv[b, :, qk + lo : qk + lo + 256] = mm(r.n1[...], fqkv[:, 2 * qk + lo : 2 * qk + lo + 256]).astype(BF16)
+
+    kvs, kvr = r.kvsem
+
+    def kv_copy(slot, which, peer):
+        return remote(kv.at[slot], kv.at[slot], kvs.at[which], kvr.at[slot], ctx=peer)
+
+    @pl.when(x == 0)
+    def _():
+        kv_copy(b, 0, p.xp).start()
+
+    @pl.when(c == 0)
+    def _():
+        kv_copy(b, 1, p.ic).start()
+
+    for i, peer in enumerate((p.ic, p.xp, p.dg)):
+        remote(r.segrow, r.segall.at[peer], segs.at[i], segr.at[peer], ctx=peer).wait_recv()
+    mask, num, den = r.mask, r.num, r.den
+    num[...] = jnp.zeros_like(num)
+    den[...] = jnp.zeros_like(den)
+    lane = lax.broadcasted_iota(jnp.int32, (1, 128), 1)
+
+    def q_of(h):
+        keep = (lane // FEAT) == h
+        return jnp.where(keep, r.q[...], jnp.zeros((), BF16))
+
+    def attend_block(j):
+        same = r.segcol[:, 0:1] == r.segall[j, 0:1, :]
+        ri = lax.broadcasted_iota(jnp.int32, (rows_here, rows_here), 0)
+        ci = lax.broadcasted_iota(jnp.int32, (rows_here, rows_here), 1)
+        reach = ri + jnp.where(j == b, 0, rows_here) >= ci
+        mask[j] = jnp.where(same & reach, 1.0, 0.0)
+
+        @pl.loop(0, heads // 2)
+        def _(pair):
+            at = pl.ds(at128(pair * 128), 128)
+            vpair = kv[j, :, pl.ds(at128(qk + pair * 128), 128)]
+            sums = []
+            for e in range(2):
+                s = mm_nt(q_of(pair * 2 + e), kv[j, :, 0:qk]) * 0.25
+                w = (1.0 + s + 0.5 * s * s) * mask[j]
+                sums.append((mm(w.astype(BF16), vpair), jnp.sum(w, axis=1, keepdims=True)))
+            low_half = lane < HEAD_V
+            num[:, at] += jnp.where(low_half, sums[0][0], sums[1][0])
+            den[:, at] += jnp.where(low_half, sums[0][1], sums[1][1])
+
+    attend_block(b)
+    advance(3.3)
+
+    @pl.when(x == 1)
+    def _():
+        kv_copy(c, 2, p.ic).wait_recv()
+        kv_copy(c, 2, p.ic).start()
+
+    @pl.when(c == 1)
+    def _():
+        kv_copy(p.ic, 1, p.ic).wait_recv()
+
+    @pl.when(x == 1)
+    def _():
+        kv_copy(1 - c, 2, p.ic).wait_recv()
+
+    @pl.loop(1, b + 1)
+    def _(m):
+        attend_block(b - m)
+
+    inv = 1.0 / den[...]
+    den[...] = inv
+    num[...] = num[...] * inv
+    r.mix[...] = num[...].astype(BF16)
+
+    ready(1, 2)
+    for ch in range(blocks):
+        y_put(0, ch, mm(r.mix[...], fo[:, ch * 256 : ch * 256 + 256]))
+    send_mix.start()
+    send_n1.start()
+    advance(4.5)
+    y_wait(0, [lambda u=u: advance(u) for u in (5.0, 5.7, 6.3)])
+
+    def norm_two(rs):
+        v = x_rows(rs) + y_rows(0, rs)
+        r.mid[rs, :] = v
+        r.n2[rs, :] = (v * rsq(v) * r.gain[1:2, :]).astype(BF16)
+
+    per_rows(norm_two)
+    send_mix.relay()
+    send_n2.start()
+
+    fchunks = -(-ffp // 256)
+
+    def per_ff(body):
+        @pl.loop(0, fchunks)
+        def _(i):
+            body(at128(jnp.minimum(i * 256, ffp - 256)))
+
+    ready(2, 6)
+    def wide(ref, off):
+        return ref[:, pl.ds(off, 256)]
+
+    def forward_ff(off):
+        g = mm(r.n2[...], wide(fg, off))
+        u = mm(r.n2[...], wide(fu, off))
+        r.g[:, pl.ds(off, 256)] = g
+        r.u[:, pl.ds(off, 256)] = u
+        sig = 1.0 / (1.0 + jnp.exp(-g))
+        r.hid[:, pl.ds(off, 256)] = (g * sig * u).astype(BF16)
+
+    per_ff(forward_ff)
+    send_hid.start()
+    ready(6, ng)
+    for ch in range(blocks):
+        y_put(1, ch, mm(r.hid[...], fd[:, ch * 256 : ch * 256 + 256]))
+    send_hid.relay()
+    get_teacher.wait()
+    small = r.small
+    small[...] = jnp.zeros_like(small)
+    y_wait(1)
+
+    def finish_forward(rs):
+        y = r.mid[rs, :] + y_rows(1, rs)
+        t = jnp.concatenate([r.tv[rs, o : o + 128] for o in order], axis=1).astype(F32)
+        m = (y - t) * r.valid[rs, 0:1]
+        r.mis[rs, :] = m
+        r.dy[rs, :] = m.astype(BF16)
+        yb = y.astype(BF16)
+        for i, o in enumerate(order):
+            r.layer_out[rs, o : o + 128] = yb[:, i * 128 : i * 128 + 128]
+        small[2:3, :] += jnp.sum(m * m, axis=0, keepdims=True)
+        small[3:4, :] += jnp.broadcast_to(jnp.sum(r.valid[rs, :], axis=0, keepdims=True)[:, 0:1], (1, width))
+
+    per_rows(finish_forward)
+    send_dy.start()
+
+    def backward_ff(off):
+        dh = mm_nt(r.dy[...], fd[pl.ds(off, 256), :])
+        g = r.g[:, pl.ds(off, 256)]
+        u = r.u[:, pl.ds(off, 256)]
+        sig = 1.0 / (1.0 + jnp.exp(-g))
+        r.dg[:, pl.ds(off, 256)] = (dh * u * sig * (1.0 + g * (1.0 - sig))).astype(BF16)
+        r.du[:, pl.ds(off, 256)] = (dh * g * sig).astype(BF16)
+
+    per_ff(backward_ff)
+    send_dg.start()
+    send_du.start()
+    for ch in range(blocks):
+        rows = slice(ch * 256, ch * 256 + 256)
+        y_put(2, ch, mm_nt(r.dg[...], fg[rows, :]) + mm_nt(r.du[...], fu[rows, :]))
+
+    red = Reduce(
+        p,
+        [r.part[i] for i in range(5)],
+        [r.seen[i] for i in range(5)],
+        [r.out_d, r.out_g, r.out_u, r.out_o, r.out_q],
+        r.rsem,
+    )
+    turned = r.turned
+
+    def turn(src):
+        w = src.shape[1]
+
+        @pl.loop(0, 4)
+        def _(i):
+            at = pl.ds(pl.multiple_of(i * rows_here, rows_here), rows_here)
+            turned[0:w, at] = jnp.transpose(src[at, :])
+
+    def grad_rows(g, rhs):
+        rows = r.part[g].shape[1]
+
+        @pl.loop(0, rhs.shape[1] // 128 // 2 if rhs.shape[1] % 256 == 0 else rhs.shape[1] // 128)
+        def _(i):
+            w = 256 if rhs.shape[1] % 256 == 0 else 128
+            at = pl.ds(at128(i * w), w)
+            res = mm(turned[0 : n * rows, :], rhs[:, at]).astype(BF16)
+            for s in range(n):
+                r.part[g][s, :, at] = res[s * rows : s * rows + rows, :]
+
+    def grad_cols(g, rhs):
+        rows = r.part[g].shape[1]
+
+        @pl.loop(0, rows // 256)
+        def _(i):
+            at = pl.ds(pl.multiple_of(i * 256, 256), 256)
+            res = mm(turned[at, :], rhs[...]).astype(BF16)
+            for s in range(n):
+                r.part[g][s, at, :] = res[:, s * 128 : s * 128 + 128]
+
+    send_hid.wait()
+    turn(r.hidx)
+    send_dy.wait()
+    grad_cols(0, r.dyc)
+    red.stage(0, 0)
+    send_n2.wait()
+    turn(r.n2c)
+    send_dg.relay()
+    send_du.relay()
+    send_dg.wait()
+    grad_rows(1, r.dgx)
+    red.stage(1, 0)
+    send_du.wait()
+    grad_rows(2, r.dux)
+    red.stage(2, 0)
+
+    y_wait(2)
+
+    def norm_back(i, row, v, base, rs):
+        dn = y_rows(i, rs)
+        inv_root = rsq(v)
+        w = dn * r.gain[row : row + 1, :]
+        small[row : row + 1, :] += jnp.sum(dn * v * inv_root, axis=0, keepdims=True)
+        m = jnp.mean(w * v, axis=1, keepdims=True)
+        return base + inv_root * w - v * (inv_root * inv_root * inv_root * m)
+
+    def middle_back(rs):
+        d = norm_back(2, 1, r.mid[rs, :], r.mis[rs, :], rs)
+        r.mis[rs, :] = d
+        r.da[rs, :] = d.astype(BF16)
+
+    per_rows(middle_back)
+    send_da.start()
+
+    dnum, dden = r.dnum, r.dden
+    for ch in range(vw // 256):
+        at = slice(ch * 256, ch * 256 + 256)
+        d = mm_nt(r.da[...], fo[at, :]) * den[:, at]
+        dnum[:, at] = d.astype(BF16)
+        dden[:, at] = d * num[:, at]
+    red.stage(0, 1)
+    dkvp, dkv, dq = r.dkvp, r.dkv, r.dqf
+    dq[...] = jnp.zeros_like(dq)
+
+    def back_block(j):
+        dkv[...] = jnp.zeros_like(dkv)
+
+        @pl.loop(0, heads // 2)
+        def _(pair):
+            at = pl.ds(at128(pair * 128), 128)
+            vat = pl.ds(at128(qk + pair * 128), 128)
+            dv = []
+            for e in range(2):
+                h = pair * 2 + e
+                qh = q_of(h)
+                keep_v = (lane // HEAD_V) == e
+                keep_q = (lane // FEAT) == h
+                s = mm_nt(qh, kv[j, :, 0:qk]) * 0.25
+                w = ((1.0 + s + 0.5 * s * s) * mask[j]).astype(BF16)
+                dn = jnp.where(keep_v, dnum[:, at], jnp.zeros((), BF16))
+                dd = jnp.sum(jnp.where(keep_v, dden[:, at], 0.0), axis=1, keepdims=True)
+                dw = mm_nt(dn, kv[j, :, vat]) - dd
+                ds = (dw * (1.0 + s) * (0.25 * mask[j])).astype(BF16)
+                dv.append(mm_tn(w, dn))
+                kh = jnp.where(keep_q, kv[j, :, 0:qk], jnp.zeros((), BF16))
+                dq[...] += mm(ds, kh)
+                dkv[:, 0:qk] += mm_tn(ds, qh)
+            dkv[:, vat] = dv[0] + dv[1]
+
+    @pl.loop(0, b)
+    def _(j):
+        back_block(j)
+        dkvp[j] = dkv[...].astype(BF16)
+
+    dks, dkr = r.dksem
+    back = r.back
+
+    def dk_copy(src, slot, which, peer):
+        return remote(src, back.at[slot], dks.at[which], dkr.at[slot], ctx=peer)
+
+    @pl.when(c == 1)
+    def _():
+        dk_copy(dkvp.at[p.ic], 0, 0, p.ic).start()
+
+    @pl.when(x == 1)
+    def _():
+        dk_copy(dkvp.at[1 - c], 1, 1, p.ic).start()
+
+    back_block(b)
+    red.stage(1, 1)
+
+    @pl.when(x == 1)
+    def _():
+        dk_copy(dkvp.at[1 - c], 1, 1, p.ic).wait_recv()
+        dkvp[b] = (dkvp[c].astype(F32) + back[1].astype(F32)).astype(BF16)
+        dk_copy(dkvp.at[b], 2, 2, p.xp).start()
+
+    @pl.when(c == 0)
+    def _():
+        dk_copy(dkvp.at[b], 0, 0, p.ic).wait_recv()
+        dkv[...] += back[0].astype(F32)
+
+    dqkv = r.dqkv
+    dqkv[:, 0:qk] = dq[...].astype(BF16)
+    send_da.wait()
+    send_mix.wait()
+    turn(r.mixx)
+    grad_cols(3, r.dac)
+    red.stage(3, 0)
+    red.stage(2, 1)
+
+    @pl.when(x == 0)
+    def _():
+        dk_copy(dkvp.at[b], 2, 2, p.xp).wait_recv()
+        dkv[...] += back[2].astype(F32)
+
+    dqkv[:, qk : 2 * qk + vw] = dkv[...].astype(BF16)
+    send_dqkv.start()
+    for ch in range(blocks):
+        y_put(3, ch, mm_nt(dqkv[...], fqkv[ch * 256 : ch * 256 + 256, :]))
+    send_n1.wait()
+    turn(r.n1c)
+    send_dqkv.relay()
+    send_dqkv.wait()
+    grad_rows(4, r.dqkvx)
+    red.stage(4, 0)
+    red.stage(0, 2)
+
+    y_wait(3)
+
+    def input_back(rs):
+        d = norm_back(3, 0, x_rows(rs), r.mis[rs, :], rs).astype(BF16)
+        for i, o in enumerate(order):
+            r.grad_in[rs, o : o + 128] = d[:, i * 128 : i * 128 + 128]
+
+    per_rows(input_back)
+
+    sms, smr = r.smsem
+    parts, lines = r.smctx, r.smz
+    for i, peer in enumerate((p.ic, p.xp, p.dg)):
+        remote(small, parts.at[b], sms.at[0, i], smr.at[0, b], ctx=peer).start()
+    parts[b] = small[...]
+    red.stage(3, 1)
+    red.last(0)
+    red.stage(1, 2)
+    for i, peer in enumerate((p.ic, p.xp, p.dg)):
+        remote(small, parts.at[peer], sms.at[0, i], smr.at[0, peer], ctx=peer).wait_recv()
+    lines[n] = parts[0] + parts[1] + parts[2] + parts[3]
+    for s in range(n):
+
+        @pl.when(z != s)
+        def _():
+            remote(lines.at[n], lines.at[z], sms.at[1, s], smr.at[1, z], fsdp=s).start()
+
+    red.last(1)
+    red.stage(4, 1)
+    red.stage(2, 2)
+    red.last(2)
+    red.relay(0)
+    red.stage(3, 2)
+    red.last(3)
+    red.stage(4, 2)
+    red.relay(1)
+    red.last(4)
+    for s in range(n):
+
+        @pl.when(z != s)
+        def _():
+            remote(lines.at[n], lines.at[s], sms.at[1, s], smr.at[1, s], fsdp=s).wait_recv()
+
+    total = jnp.zeros_like(small)
+    for s in range(n):
+        total += jnp.where(z == s, lines[n], lines[s])
+    for i, o in enumerate(order):
+        r.sums[:, o : o + 128] = total[:, i * 128 : i * 128 + 128]
+    red.relay(2)
+    red.relay(3)
+    red.relay(4)
+    for g in range(5):
+        red.finish(g)
+
+    gather.drain()
+    for k in (send_n1, send_da, send_n2, send_dy, send_hid, send_dg, send_du, send_mix, send_dqkv):
+        k.drain()
+    for i in range(4):
+        for ch in range(blocks):
+            y_copy(i, ch).wait_send()
+    for s in range(n):
+
+        @pl.when(z != s)
+        def _():
+            remote(r.gains, gath.at[z], gsend.at[s], grecv.at[z], fsdp=s).wait_send()
+            remote(lines.at[n], lines.at[z], sms.at[1, s], smr.at[1, z], fsdp=s).wait_send()
+
+    for i, peer in enumerate((p.ic, p.xp, p.dg)):
+        remote(r.segrow, r.segall.at[b], segs.at[i], segr.at[b], ctx=peer).wait_send()
+        remote(small, parts.at[b], sms.at[0, i], smr.at[0, b], ctx=peer).wait_send()
+
+    @pl.when(x == 0)
+    def _():
+        kv_copy(b, 0, p.xp).wait_send()
+
+    @pl.when(c == 0)
+    def _():
+        kv_copy(b, 1, p.ic).wait_send()
+
+    @pl.when(x == 1)
+    def _():
+        kv_copy(c, 2, p.ic).wait_send()
+        dk_copy(dkvp.at[1 - c], 1, 1, p.ic).wait_send()
+        dk_copy(dkvp.at[b], 2, 2, p.xp).wait_send()
+
+    @pl.when(c == 1)
+    def _():
+        dk_copy(dkvp.at[p.ic], 0, 0, p.ic).wait_send()
+
+
+def mega(n, layer_in, segment_ids, valid_mask, teacher, attn_gain, w_query, w_key, w_value, w_out, ffn_gain, w_gate, w_up, w_down):
+    x = layer_in[0]
+    rows, width = x.shape
+    qk, vw, ff = w_query.shape[1], w_value.shape[1], w_gate.shape[1]
+    ffp = up_to(ff, 128)
+    fh = up_to(ffp // 2, 256)
+    half_d = width // 2
+    blocks = width // 256
+    seg = segment_ids[0].astype(F32)
+    inputs = dict(
+        x=x,
+        teacher=teacher[0],
+        wq=w_query,
+        wk=w_key,
+        wv=w_value,
+        wo=w_out,
+        wg=jnp.pad(w_gate, ((0, 0), (0, ffp - ff))),
+        wu=jnp.pad(w_up, ((0, 0), (0, ffp - ff))),
+        wd=w_down,
+        gains=jnp.concatenate(
+            [attn_gain[None], ffn_gain[None], jnp.zeros((6, attn_gain.shape[0]), BF16)], axis=0
+        ).astype(F32),
+        segrow=jnp.broadcast_to(seg[None, :], (8, rows)),
+        segcol=jnp.broadcast_to(seg[:, None], (rows, 128)),
+        valid=jnp.broadcast_to(valid_mask[0].astype(F32)[:, None], (rows, 128)),
+    )
+    hbm = list(inputs)[:9]
+    outs = dict(
+        layer_out=((rows, width), BF16),
+        grad_in=((rows, width), BF16),
+        out_d=((4, fh, 128), BF16),
+        out_g=((4, 128, fh), BF16),
+        out_u=((4, 128, fh), BF16),
+        out_o=((4, vw // 2, 128), BF16),
+        out_q=((4, 128, (2 * qk + vw) // 2), BF16),
+        sums=((8, width), F32),
+    )
+    dma = pltpu.SemaphoreType.DMA
+    ng = 8
+    vm = pltpu.VMEM
+    piece = [(fh, 128), (128, fh), (128, fh), (vw // 2, 128), (128, (2 * qk + vw) // 2)]
+    scratch = dict(
+        lsem=dma((20,)),
+        gs=[dma((ng, n)) for _ in range(9)],
+        gnsem=[dma((n,)), dma((n,))],
+        segsem=[dma((3,)), dma((4,))],
+        csem=[dma((4, 3)), dma((4, 4))],
+        hsem=[dma((5, 3)), dma((5, 4))],
+        ysem=[dma((4, blocks)), dma((4, blocks))],
+        kvsem=[dma((3,)), dma((4,))],
+        dksem=[dma((3,)), dma((3,))],
+        rsem=[dma((5, n)), dma((5, n + 1)), dma((5, 3)), dma((5, 4))],
+        smsem=[dma((2, max(n, 3))), dma((2, max(n, 4)))],
+        fqkv=vm((width, 2 * qk + vw), BF16),
+        fo=vm((vw, width), BF16),
+        fg=vm((width, ffp), BF16),
+        fu=vm((width, ffp), BF16),
+        fd=vm((ffp, width), BF16),
+        xv=vm((rows, width), BF16),
+        tv=vm((rows, width), BF16),
+        gath=vm((n, 8, width // n), F32),
+        gain=vm((8, width), F32),
+        segall=vm((4, 8, rows), F32),
+        n1=vm((rows, width), BF16),
+        n2=vm((rows, width), BF16),
+        dy=vm((rows, width), BF16),
+        da=vm((rows, width), BF16),
+        n1c=vm((4 * rows, half_d), BF16),
+        n2c=vm((4 * rows, half_d), BF16),
+        dyc=vm((4 * rows, half_d), BF16),
+        dac=vm((4 * rows, half_d), BF16),
+        hid=vm((rows, ffp), BF16),
+        dg=vm((rows, ffp), BF16),
+        du=vm((rows, ffp), BF16),
+        mix=vm((rows, vw), BF16),
+        dqkv=vm((rows, 2 * qk + vw), BF16),
+        hidx=vm((4 * rows, fh), BF16),
+        dgx=vm((4 * rows, fh), BF16),
+        dux=vm((4 * rows, fh), BF16),
+        mixx=vm((4 * rows, vw // 2), BF16),
+        dqkvx=vm((4 * rows, (2 * qk + vw) // 2), BF16),
+        ysend=vm((4, blocks, rows, 256), BF16),
+        yrecv=vm((4, blocks, rows, 256), BF16),
+        q=vm((rows, qk), BF16),
+        kv=vm((4, rows, qk + vw), BF16),
+        mask=vm((4, rows, rows), F32),
+        num=vm((rows, vw), F32),
+        den=vm((rows, vw), F32),
+        mid=vm((rows, width), F32),
+        mis=vm((rows, width), F32),
+        g=vm((rows, ffp), F32),
+        u=vm((rows, ffp), F32),
+        small=vm((8, width), F32),
+        smctx=vm((4, 8, width), F32),
+        smz=vm((n + 1, 8, width), F32),
+        dnum=vm((rows, vw), BF16),
+        dden=vm((rows, vw), F32),
+        dqf=vm((rows, qk), F32),
+        dkv=vm((rows, qk + vw), F32),
+        dkvp=vm((4, rows, qk + vw), BF16),
+        back=vm((3, rows, qk + vw), BF16),
+        turned=vm((max(fh, half_d), 4 * rows), BF16),
+        part=[vm((n,) + s, BF16) for s in piece],
+        seen=[vm((n + 1,) + s, BF16) for s in piece],
+    )
+    flat, layout = [], []
+    for k, v in scratch.items():
+        if isinstance(v, list):
+            layout.append((k, len(v)))
+            flat.extend(v)
+        else:
+            layout.append((k, 0))
+            flat.append(v)
+
+    def kernel(*refs):
+        names = list(inputs) + list(outs)
+        bound = list(refs[: len(names)])
+        at = len(names)
+        for k, count in layout:
+            names.append(k)
+            if count:
+                bound.append(refs[at : at + count])
+                at += count
+            else:
+                bound.append(refs[at])
+                at += 1
+        mega_kernel(n, names, *bound)
+
+    res = pl.pallas_call(
+        kernel,
+        out_shape=[jax.ShapeDtypeStruct(*v) for v in outs.values()],
+        in_specs=[pl.BlockSpec(memory_space=pl.ANY if k in hbm else pltpu.VMEM) for k in inputs],
+        out_specs=[pl.BlockSpec(memory_space=pltpu.VMEM)] * len(outs),
+        scratch_shapes=flat,
+        compiler_params=pltpu.CompilerParams(
+            collective_id=0, has_side_effects=True, vmem_limit_bytes=67043328
+        ),
+        name="block_step",
+    )(*inputs.values())
+    o = SimpleNamespace(**dict(zip(outs, res)))
+
+    def rows_of(a, total):
+        w = a.shape[2]
+        keep = total - w
+        return jnp.concatenate(
+            [jnp.concatenate([a[cc], a[2 + cc][:, w - (up_to(total, 128) - w) : w - (up_to(total, 128) - total)]], axis=1) for cc in range(2)],
+            axis=0,
+        ).astype(F32)
+
+    def cols_of(a, total):
+        w = a.shape[1]
+        return jnp.concatenate(
+            [jnp.concatenate([a[cc], a[2 + cc][w - (up_to(total, 128) - w) : w - (up_to(total, 128) - total)]], axis=0) for cc in range(2)],
+            axis=1,
+        ).astype(F32)
+
+    gq = rows_of(o.out_q, 2 * qk + vw)
+    lo = lax.axis_index("fsdp") * (width // n)
+    mine = lax.dynamic_slice_in_dim(o.sums, lo, width // n, axis=1)
+    loss = jnp.sum(o.sums[2]) / (o.sums[3, 0] * width)
+    return (
+        o.layer_out[None],
+        o.grad_in[None],
+        mine[0],
+        gq[:, :qk],
+        gq[:, qk : 2 * qk],
+        gq[:, 2 * qk :],
+        cols_of(o.out_o, vw),
+        mine[1],
+        rows_of(o.out_g, ff),
+        rows_of(o.out_u, ff),
+        cols_of(o.out_d, ff),
+        loss,
+    )
+
+
+def per_device(*arrays):
+    n = lax.axis_size("fsdp")
+    layer_in, w_query, w_value = arrays[0], arrays[5], arrays[7]
+    fits = (
+        lax.axis_size("ctx") == 4
+        and lax.axis_size("tp") == 2
+        and layer_in.shape[0] == 1
+        and w_query.shape[0] == 256
+        and w_query.shape[1] == 128
+        and w_value.shape[1] % 512 == 0
+        and layer_in.shape[1] % 256 == 0
+    )
+    return mega(n, *arrays) if fits else general(*arrays)
+
+
 def solution(mesh):
     placed = (
         P("fsdp", "ctx", None),

time: 844 us -> 251 us (0.30); the launches traced: 835 us -> 251 us
  waiting for transfers between devices: 532 us -> 0 us
  Pallas kernels: 0 us -> 226 us
  blocking collectives: 118 us -> 0 us
  matrix products: 83.8 us -> 0 us
  other arithmetic: 33.4 us -> 6.51 us
  between operations: 19.7 us -> 3.23 us
  local copies, waits for them, and re-layouts: 27.4 us -> 14.8 us
  starting transfers between devices: 12.1 us -> 0 us
    pallas_call x0 -> x1, Pallas kernels: none -> 226 us  [mega(): pl.pallas_call(kernel, out_shape=[jax.ShapeDtypeStruct(*v) for v in outs....]
    reduce_scatter x7 -> x0, waiting for transfers between devices: 224 us -> none  [the longest x1 57.2 us: per_device(): lax.psum_scatter(grad_gate.astype(jnp.bfloat16), 'fsdp', scatter_dimensio...]
    all_gather x7 -> x0, waiting for transfers between devices: 169 us -> none  [the longest x1 57.8 us: per_device(): lax.all_gather(w_gate, 'fsdp', axis=0, tiled=True)]
    psum x5 -> x0, waiting for transfers between devices: 136 us -> none  [the longest x2 76.7 us: tp_forward(): return lax.psum(partial_sum, 'tp')]
    dot_general x35 -> x0, matrix products: 83.8 us -> none  [the longest x7 19.4 us: product(): return jnp.dot(left_side, right_side, preferred_element_type=jnp.float32)]
    all_gather x6 -> x0, blocking collectives: 63.9 us -> none  [the longest x1 16.3 us: per_device(): lax.all_gather(w_key, 'fsdp', axis=0, tiled=True)]
    psum x2 -> x0, blocking collectives: 38.7 us -> none  [the longest x1 32.4 us: per_device(): total_sq, total_valid = lax.psum((sum_squares, sum_valid), ('fsdp', 'ctx'))]
    unnamed x2 -> x0, blocking collectives: 14.9 us -> none
  transfers between devices with their start and end apart: 19 -> 0, of which waited for: 15 -> 0; matrix products, arithmetic and copies ran while one was open for 11% -> 0% of each run, Pallas kernels for 0% -> 0%
where the time goes in v2:
time: 251 us
  Pallas kernels  226 us (90%)
  local copies, waits for them, and re-layouts  14.8 us (6%)
  other arithmetic  6.51 us (3%)
  between operations  3.23 us (1%)
    pallas_call x1, Pallas kernels, mega(): pl.pallas_call(kernel, out_shape=[jax.ShapeDtypeStruct(*v) for v in outs....  226 us
    unnamed x24, local copies, waits for them, and re-layouts  6.45 us

profile of v2, /device:TPU:0, one launch (start us, length us, event | category | flops | bytes accessed | tf_op | source)
XLA Modules:
  0.0 250.9 jit_solution(8817712775542947518)
XLA Ops:
  0.6 0.7 convert_element_type.41
  1.3 0.8 broadcast_in_dim.40.refs_11_
  2.1 0.6 broadcast_in_dim.39.refs_10_
  2.7 1.4 copy.25
  4.1 0.9 pad.7.refs_6_
  5.0 0.0 copy-done
  5.1 0.3 copy.26
  5.4 0.9 pad.8.refs_7_
  6.3 0.0 copy-done.6
  6.3 0.8 broadcast_in_dim.41.refs_12_
  7.1 0.0 copy-done.7
  7.1 0.1 pad.31.clone
  7.2 0.7 maximum_convert_fusion.6.refs_9_
  7.9 226.3 %block_step.1 = (bf16[256,1024]{1,0:T(8,128)(2,1)}, bf16[256,1024]{1,0:T(8,128)(2,1)}, bf16[4,768,128]{2,1,0:T(8,128)(2,1)}, bf16[4,128,768]{2,1,0:T(8,128)(2,1)...) custom-call(bf16[256,1024]{1,0:T(8,128)(2,1)} %bitcast.51, ...), custom_call_target="tpu_custom_call" | custom-call | tf_op jit(solution)/shard_map/block_step/pallas_call | solution.py:1406
  234.2 1.6 slice_bitcast_fusion.5
  235.8 0.1 maximum_convert_fusion.1
  235.9 1.5 copy.28
  237.5 0.1 maximum_convert_fusion
  237.6 1.5 copy.27
  239.1 0.0 copy-done.4
  239.2 0.7 maximum_convert_fusion.4
  239.9 0.9 fusion.1
  240.8 0.0 copy-done.5
  240.8 0.8 maximum_convert_fusion.3
  241.7 1.2 maximum_convert_fusion.2
  242.9 1.2 slice.135
  244.7 1.4 slice_reduce_fusion
  246.8 1.4 fusion.2
  248.2 0.0 copy-done.3
  248.2 0.8 copy.31
  249.0 0.0 copy-done.2
  249.0 0.8 copy.32
  (23 shorter events, 0.2 us)
Async XLA Ops:
  2.1 3.0 %copy-start = (bf16[256,1376]{0,1:T(8,128)(2,1)S(1)}, bf16[256,1376]{0,1:T(8,128)(2,1)}, u32[]{:S(2)}) copy-start(bf16[256,1376]{0,1:T(8,128)(2,1)} %param.24) | copy-start | bytes 2113540
  5.0 1.3 copy-start.6
  5.1 2.0 copy-start.7
  5.1 2.0 copy-start.8
  237.6 1.5 copy-start.4
  239.1 1.6 copy-start.5
  239.2 2.4 copy-start.1
  241.6 6.5 %copy-start.3 = (bf16[256,1024]{1,0:T(8,128)(2,1)S(1)}, bf16[256,1024]{1,0:T(8,128)(2,1)}, u32[]{:S(2)}) copy-start(bf16[256,1024]{1,0:T(8,128)(2,1)} %get-tuple-element.20) | copy-start | bytes 1572868
  241.7 7.3 %copy-start.2 = (bf16[256,1024]{1,0:T(8,128)(2,1)S(1)}, bf16[256,1024]{1,0:T(8,128)(2,1)}, u32[]{:S(2)}) copy-start(bf16[256,1024]{1,0:T(8,128)(2,1)} %get-tuple-element.21) | copy-start | bytes 1572868

commit v3 on v2

--- a/solution.py
+++ b/solution.py
@@ -521,11 +521,12 @@
 
 
 class Reduce:
-    def __init__(self, p, parts, seen, done, sems):
+    def __init__(self, p, parts, seen, done, other, sems):
         self.p = p
         self.parts = parts
         self.seen = seen
         self.done = done
+        self.other = other
         (self.ss, self.rs, self.fs, self.fr) = sems
 
     def move(self, g, s, slot, to):
@@ -536,9 +537,17 @@
     def arrived(self, g, slot):
         self.move(g, 0, slot, self.p.z).wait_recv()
 
+    def by_rows(self, g, body):
+        @pl.loop(0, self.parts[g].shape[1] // 128)
+        def _(i):
+            body(pl.ds(at128(i * 128), 128))
+
     def add(self, g, s, slot):
-        total = self.parts[g][s].astype(F32) + self.seen[g][slot].astype(F32)
-        self.parts[g][s] = total.astype(BF16)
+        def body(at):
+            total = self.parts[g][s, at, :].astype(F32) + self.seen[g][slot, at, :].astype(F32)
+            self.parts[g][s, at, :] = total.astype(BF16)
+
+        self.by_rows(g, body)
 
     def stage(self, g, k):
         p = self.p
@@ -575,27 +584,70 @@
             self.arrived(g, n)
             self.add(g, p.z, n)
 
-        self.done[g][p.b] = self.parts[g][p.z]
-        self.spread(g, p.b, 0, p.ic).start()
-        self.spread(g, p.b, 1, p.xp).start()
-
-    def spread(self, g, slot, which, to):
-        return remote(
-            self.done[g].at[slot], self.done[g].at[slot], self.fs.at[g, which], self.fr.at[g, slot], ctx=to
-        )
+        if self.other[g] is not None:
+            self.across(g).start()
+            return
+        self.block(g, p.x, p.c)[...] = self.mine(g)[...]
+        self.spread(g, p.b, 0, p.ic, self.mine(g)).start()
+        self.spread(g, p.b, 1, p.xp, self.mine(g)).start()
+
+    def mine(self, g):
+        p = self.p
+        half = self.done[g].shape[0] // 2
+        skip = self.parts[g].shape[1] - half
+        return self.parts[g].at[p.z, pl.ds(pl.multiple_of(p.x * skip, 16), half), :]
+
+    def block(self, g, x, c):
+        half = self.done[g].shape[0] // 2
+        return self.done[g].at[pl.ds(pl.multiple_of(x * half, 16), half), pl.ds(at128(c * 128), 128)]
+
+    def spread(self, g, slot, which, to, src=None):
+        dst = self.block(g, slot // 2, slot % 2)
+        return remote(dst if src is None else src, dst, self.fs.at[g, which], self.fr.at[g, slot], ctx=to)
+
+    def side(self, g, c):
+        at = pl.ds(at128(c * 128), 128)
+        if self.done[g].shape[1] == 256:
+            return self.done[g].at[:, at]
+        return self.done[g].at[at, :]
+
+    def across(self, g):
+        p = self.p
+        return remote(self.parts[g].at[p.z], self.other[g], self.fs.at[g, 0], self.fr.at[g, 0], ctx=p.xp)
+
+    def beside(self, g, c):
+        ref = self.side(g, c)
+        return remote(ref, ref, self.fs.at[g, 1], self.fr.at[g, 1], ctx=self.p.ic)
 
     def relay(self, g):
         p = self.p
+        if self.other[g] is not None:
+            self.across(g).wait_recv()
+
+            side = self.side(g, p.c)
+
+            def body(at):
+                total = self.parts[g][p.z, at, :].astype(F32) + self.other[g][at, :].astype(F32)
+                side[at, :] = total.astype(BF16)
+
+            self.by_rows(g, body)
+            self.beside(g, p.c).start()
+            return
         self.spread(g, p.xp, 1, p.xp).wait_recv()
         self.spread(g, p.xp, 2, p.ic).start()
 
     def finish(self, g):
         p = self.p
-        self.spread(g, p.ic, 0, p.ic).wait_recv()
-        self.spread(g, p.dg, 2, p.ic).wait_recv()
-        self.spread(g, p.b, 0, p.ic).wait_send()
-        self.spread(g, p.b, 1, p.xp).wait_send()
-        self.spread(g, p.xp, 2, p.ic).wait_send()
+        if self.other[g] is not None:
+            self.beside(g, 1 - p.c).wait_recv()
+            self.beside(g, p.c).wait_send()
+            self.across(g).wait_send()
+        else:
+            self.spread(g, p.ic, 0, p.ic).wait_recv()
+            self.spread(g, p.dg, 2, p.ic).wait_recv()
+            self.spread(g, p.b, 0, p.ic, self.mine(g)).wait_send()
+            self.spread(g, p.b, 1, p.xp, self.mine(g)).wait_send()
+            self.spread(g, p.xp, 2, p.ic).wait_send()
 
         @pl.loop(0, p.n)
         def _(s):
@@ -638,6 +690,41 @@
         p = self.p
         for which, peer in enumerate((p.xp, p.dg, p.ic)):
             self.copy(peer, which).wait_send()
+
+
+class Pair:
+    def __init__(self, p, k, src, dst, sems):
+        self.p = p
+        self.k = k
+        self.src = src
+        self.dst = dst
+        self.send, self.recv = sems
+
+    def slot(self, c):
+        rows = self.src.shape[0]
+        return self.dst.at[pl.ds(pl.multiple_of(c * rows, rows), rows), :]
+
+    def part(self, c):
+        w = self.dst.shape[1]
+        if w == self.src.shape[1]:
+            return self.src
+        return self.src.at[:, pl.ds(at128(c * w), w)]
+
+    def copy(self):
+        p = self.p
+        return remote(self.part(1 - p.c), self.slot(p.c), self.send.at[self.k], self.recv.at[self.k], ctx=p.ic)
+
+    def start(self):
+        c = self.p.c
+        self.copy().start()
+        self.slot(c)[...] = self.part(c)[...]
+
+    def wait(self):
+        p = self.p
+        remote(self.part(1 - p.c), self.slot(1 - p.c), self.send.at[self.k], self.recv.at[self.k], ctx=p.ic).wait_recv()
+
+    def drain(self):
+        self.copy().wait_send()
 
 
 class Halves:
@@ -722,15 +809,10 @@
     for cc in range(2):
         cols = pl.ds(at128((cc * n + z) * 128), 128)
         need.setdefault("o", []).append(bring(r.wo.at[:, cc * 128 : cc * 128 + 128], fo.at[:, cols]))
-    for cc in range(2):
-        rows = pl.ds(at128((cc * n + z) * 128), 128)
-        need.setdefault("g", []).append(bring(r.wg.at[cc * 128 : cc * 128 + 128, :], fg.at[rows, :]))
-        need.setdefault("u", []).append(bring(r.wu.at[cc * 128 : cc * 128 + 128, :], fu.at[rows, :]))
-    for cc in range(2):
-        cols = pl.ds(at128((cc * n + z) * 128), 128)
-        need.setdefault("d", []).append(
-            bring(r.wd.at[:, cc * 128 : cc * 128 + 128], fd.at[0:ff, cols])
-        )
+    for key, src, dst in (("g", r.wg, fg), ("u", r.wu, fu), ("d", r.wd, fd)):
+        for cc in range(2):
+            cols = pl.ds(at128((cc * n + z) * 128), 128)
+            need.setdefault(key, []).append(bring(src.at[:, cc * 128 : cc * 128 + 128], dst.at[0:ff, cols]))
     get_teacher = bring(r.teacher, r.tv)
 
     pieces, first = [], []
@@ -743,8 +825,8 @@
     for key, ref, kind, total, parts in (
         ("qkv", fqkv, "row", 64, 1),
         ("o", fo, "col", vw // 2, 1),
-        ("g", fg, "row", 64, 2),
-        ("u", fu, "row", 64, 2),
+        ("g", fg, "col", ff // 2, 2),
+        ("u", fu, "col", ff // 2, 2),
         ("d", fd, "col", ff // 2, 2),
     ):
         for i, (lo, size) in enumerate(split(total, parts)):
@@ -762,6 +844,15 @@
     own(0)
     own(1)
 
+    r.gains[...] = jnp.concatenate(
+        [r.attn_gain[...].astype(F32).reshape(1, -1), r.ffn_gain[...].astype(F32).reshape(1, -1)]
+        + [jnp.zeros((6, width // n), F32)],
+        axis=0,
+    )
+    segment = r.segment[...].astype(F32)
+    r.segrow[...] = jnp.broadcast_to(segment, (8, rows_here))
+    r.segcol[...] = jnp.transpose(jnp.broadcast_to(segment, (128, rows_here)))
+    r.valid[...] = jnp.transpose(jnp.broadcast_to(r.real[...].astype(F32), (128, rows_here)))
     gsend, grecv, gath = r.gnsem[0], r.gnsem[1], r.gath
     for s in range(n):
 
@@ -777,7 +868,8 @@
 
     pad = ffp - ff
     if pad:
-        fd[ff:ffp, :] = jnp.zeros((pad, width), BF16)
+        for ref in (fg, fu, fd):
+            ref[ff:ffp, :] = jnp.zeros((pad, width), BF16)
 
     for s in range(n):
 
@@ -814,16 +906,16 @@
         for g in range(g_from, g_to):
             gather.finish(g)
 
-    send_n1 = Columns(p, 0, r.n1, r.n1c, r.csem)
-    send_da = Columns(p, 1, r.da, r.dac, r.csem)
-    send_n2 = Columns(p, 2, r.n2, r.n2c, r.csem)
-    send_dy = Columns(p, 3, r.dy, r.dyc, r.csem)
-    fh = r.hidx.shape[1]
-    send_hid = Halves(p, 0, r.hid, r.hidx, ffp - fh, r.hsem)
-    send_dg = Halves(p, 1, r.dg, r.dgx, ffp - fh, r.hsem)
-    send_du = Halves(p, 2, r.du, r.dux, ffp - fh, r.hsem)
-    send_mix = Halves(p, 3, r.mix, r.mixx, vw // 2, r.hsem)
-    send_dqkv = Halves(p, 4, r.dqkv, r.dqkvx, (2 * qk + vw) // 2, r.hsem)
+    send_n1 = Pair(p, 0, r.n1, r.n1c, r.psem)
+    send_da = Pair(p, 1, r.da, r.dac, r.psem)
+    send_dy = Pair(p, 2, r.dy, r.dyc, r.psem)
+    send_hid = Pair(p, 3, r.hid, r.hidx, r.psem)
+    send_mix = Pair(p, 4, r.mix, r.mixx, r.psem)
+    send_dqkv = Pair(p, 5, r.dqkv, r.dqkvx, r.psem)
+    send_n2 = Columns(p, 0, r.n2, r.n2c, r.csem)
+    fh = r.dgx.shape[1]
+    send_dg = Halves(p, 0, r.dg, r.dgx, ffp - fh, r.hsem)
+    send_du = Halves(p, 1, r.du, r.dux, ffp - fh, r.hsem)
     ysend, yrecv = r.ysend, r.yrecv
 
     def y_copy(i, ch):
@@ -957,8 +1049,6 @@
         r.n2[rs, :] = (v * rsq(v) * r.gain[1:2, :]).astype(BF16)
 
     per_rows(norm_two)
-    send_mix.relay()
-    send_n2.start()
 
     fchunks = -(-ffp // 256)
 
@@ -968,12 +1058,13 @@
             body(at128(jnp.minimum(i * 256, ffp - 256)))
 
     ready(2, 6)
+
     def wide(ref, off):
-        return ref[:, pl.ds(off, 256)]
+        return ref[pl.ds(off, 256), :]
 
     def forward_ff(off):
-        g = mm(r.n2[...], wide(fg, off))
-        u = mm(r.n2[...], wide(fu, off))
+        g = mm_nt(r.n2[...], wide(fg, off))
+        u = mm_nt(r.n2[...], wide(fu, off))
         r.g[:, pl.ds(off, 256)] = g
         r.u[:, pl.ds(off, 256)] = u
         sig = 1.0 / (1.0 + jnp.exp(-g))
@@ -984,7 +1075,7 @@
     ready(6, ng)
     for ch in range(blocks):
         y_put(1, ch, mm(r.hid[...], fd[:, ch * 256 : ch * 256 + 256]))
-    send_hid.relay()
+    send_n2.start()
     get_teacher.wait()
     small = r.small
     small[...] = jnp.zeros_like(small)
@@ -1017,14 +1108,15 @@
     send_dg.start()
     send_du.start()
     for ch in range(blocks):
-        rows = slice(ch * 256, ch * 256 + 256)
-        y_put(2, ch, mm_nt(r.dg[...], fg[rows, :]) + mm_nt(r.du[...], fu[rows, :]))
+        cols = slice(ch * 256, ch * 256 + 256)
+        y_put(2, ch, mm(r.dg[...], fg[:, cols]) + mm(r.du[...], fu[:, cols]))
 
     red = Reduce(
         p,
         [r.part[i] for i in range(5)],
         [r.seen[i] for i in range(5)],
         [r.out_d, r.out_g, r.out_u, r.out_o, r.out_q],
+        [r.other[0], None, None, r.other[1], r.other[2]],
         r.rsem,
     )
     turned = r.turned
@@ -1032,7 +1124,7 @@
     def turn(src):
         w = src.shape[1]
 
-        @pl.loop(0, 4)
+        @pl.loop(0, src.shape[0] // rows_here)
         def _(i):
             at = pl.ds(pl.multiple_of(i * rows_here, rows_here), rows_here)
             turned[0:w, at] = jnp.transpose(src[at, :])
@@ -1044,17 +1136,17 @@
         def _(i):
             w = 256 if rhs.shape[1] % 256 == 0 else 128
             at = pl.ds(at128(i * w), w)
-            res = mm(turned[0 : n * rows, :], rhs[:, at]).astype(BF16)
+            res = mm(turned[0 : n * rows, 0 : rhs.shape[0]], rhs[:, at]).astype(BF16)
             for s in range(n):
                 r.part[g][s, :, at] = res[s * rows : s * rows + rows, :]
 
     def grad_cols(g, rhs):
         rows = r.part[g].shape[1]
 
-        @pl.loop(0, rows // 256)
+        @pl.loop(0, -(-rows // 256))
         def _(i):
-            at = pl.ds(pl.multiple_of(i * 256, 256), 256)
-            res = mm(turned[at, :], rhs[...]).astype(BF16)
+            at = pl.ds(at128(jnp.minimum(i * 256, rows - 256)), 256)
+            res = mm(turned[at, 0 : rhs.shape[0]], rhs[...]).astype(BF16)
             for s in range(n):
                 r.part[g][s, at, :] = res[:, s * 128 : s * 128 + 128]
 
@@ -1063,16 +1155,7 @@
     send_dy.wait()
     grad_cols(0, r.dyc)
     red.stage(0, 0)
-    send_n2.wait()
-    turn(r.n2c)
     send_dg.relay()
-    send_du.relay()
-    send_dg.wait()
-    grad_rows(1, r.dgx)
-    red.stage(1, 0)
-    send_du.wait()
-    grad_rows(2, r.dux)
-    red.stage(2, 0)
 
     y_wait(2)
 
@@ -1091,6 +1174,12 @@
 
     per_rows(middle_back)
     send_da.start()
+    send_du.relay()
+    send_n2.wait()
+    send_dg.wait()
+    turn(r.dgx)
+    grad_cols(1, r.n2c)
+    red.stage(1, 0)
 
     dnum, dden = r.dnum, r.dden
     for ch in range(vw // 256):
@@ -1098,7 +1187,6 @@
         d = mm_nt(r.da[...], fo[at, :]) * den[:, at]
         dnum[:, at] = d.astype(BF16)
         dden[:, at] = d * num[:, at]
-    red.stage(0, 1)
     dkvp, dkv, dq = r.dkvp, r.dkv, r.dqf
     dq[...] = jnp.zeros_like(dq)
 
@@ -1147,7 +1235,6 @@
         dk_copy(dkvp.at[1 - c], 1, 1, p.ic).start()
 
     back_block(b)
-    red.stage(1, 1)
 
     @pl.when(x == 1)
     def _():
@@ -1162,12 +1249,17 @@
 
     dqkv = r.dqkv
     dqkv[:, 0:qk] = dq[...].astype(BF16)
+    send_du.wait()
+    turn(r.dux)
+    grad_cols(2, r.n2c)
+    red.stage(2, 0)
+    red.stage(0, 1)
     send_da.wait()
     send_mix.wait()
     turn(r.mixx)
     grad_cols(3, r.dac)
     red.stage(3, 0)
-    red.stage(2, 1)
+    red.stage(1, 1)
 
     @pl.when(x == 0)
     def _():
@@ -1180,11 +1272,12 @@
         y_put(3, ch, mm_nt(dqkv[...], fqkv[ch * 256 : ch * 256 + 256, :]))
     send_n1.wait()
     turn(r.n1c)
-    send_dqkv.relay()
     send_dqkv.wait()
     grad_rows(4, r.dqkvx)
     red.stage(4, 0)
     red.stage(0, 2)
+    red.stage(2, 1)
+    red.last(0)
 
     y_wait(3)
 
@@ -1201,7 +1294,6 @@
         remote(small, parts.at[b], sms.at[0, i], smr.at[0, b], ctx=peer).start()
     parts[b] = small[...]
     red.stage(3, 1)
-    red.last(0)
     red.stage(1, 2)
     for i, peer in enumerate((p.ic, p.xp, p.dg)):
         remote(small, parts.at[peer], sms.at[0, i], smr.at[0, peer], ctx=peer).wait_recv()
@@ -1231,13 +1323,21 @@
     total = jnp.zeros_like(small)
     for s in range(n):
         total += jnp.where(z == s, lines[n], lines[s])
-    for i, o in enumerate(order):
-        r.sums[:, o : o + 128] = total[:, i * 128 : i * 128 + 128]
+    r.gain[...] = total
+    for cc in range(2):
+        at = pl.ds(at128((cc * n + z) * 128), 128)
+        r.grad_attn[0:1, cc * 128 : cc * 128 + 128] = r.gain[0:1, at]
+        r.grad_ffn[0:1, cc * 128 : cc * 128 + 128] = r.gain[1:2, at]
+    r.loss[...] = jnp.sum(total[2:3, :], axis=1, keepdims=True) / (total[3:4, 0:1] * width)
     red.relay(2)
     red.relay(3)
     red.relay(4)
-    for g in range(5):
+    for g in (4, 0, 1, 2, 3):
         red.finish(g)
+        if g == 4:
+            r.grad_q[...] = r.out_q[:, 0:qk].astype(F32)
+            r.grad_k[...] = r.out_q[:, qk : 2 * qk].astype(F32)
+            r.grad_v[...] = r.out_q[:, 2 * qk : 2 * qk + vw].astype(F32)
 
     gather.drain()
     for k in (send_n1, send_da, send_n2, send_dy, send_hid, send_dg, send_du, send_mix, send_dqkv):
@@ -1283,7 +1383,6 @@
     fh = up_to(ffp // 2, 256)
     half_d = width // 2
     blocks = width // 256
-    seg = segment_ids[0].astype(F32)
     inputs = dict(
         x=x,
         teacher=teacher[0],
@@ -1291,38 +1390,41 @@
         wk=w_key,
         wv=w_value,
         wo=w_out,
-        wg=jnp.pad(w_gate, ((0, 0), (0, ffp - ff))),
-        wu=jnp.pad(w_up, ((0, 0), (0, ffp - ff))),
+        wg=w_gate.T,
+        wu=w_up.T,
         wd=w_down,
-        gains=jnp.concatenate(
-            [attn_gain[None], ffn_gain[None], jnp.zeros((6, attn_gain.shape[0]), BF16)], axis=0
-        ).astype(F32),
-        segrow=jnp.broadcast_to(seg[None, :], (8, rows)),
-        segcol=jnp.broadcast_to(seg[:, None], (rows, 128)),
-        valid=jnp.broadcast_to(valid_mask[0].astype(F32)[:, None], (rows, 128)),
+        attn_gain=attn_gain,
+        ffn_gain=ffn_gain,
+        segment=segment_ids,
+        real=valid_mask,
     )
     hbm = list(inputs)[:9]
     outs = dict(
         layer_out=((rows, width), BF16),
         grad_in=((rows, width), BF16),
-        out_d=((4, fh, 128), BF16),
-        out_g=((4, 128, fh), BF16),
-        out_u=((4, 128, fh), BF16),
-        out_o=((4, vw // 2, 128), BF16),
-        out_q=((4, 128, (2 * qk + vw) // 2), BF16),
-        sums=((8, width), F32),
+        out_d=((ffp, width // n), BF16),
+        out_g=((ffp, width // n), BF16),
+        out_u=((ffp, width // n), BF16),
+        out_o=((vw, width // n), BF16),
+        grad_q=((width // n, qk), F32),
+        grad_k=((width // n, qk), F32),
+        grad_v=((width // n, vw), F32),
+        grad_attn=((1, width // n), F32),
+        grad_ffn=((1, width // n), F32),
+        loss=((1, 1), F32),
     )
     dma = pltpu.SemaphoreType.DMA
     ng = 8
     vm = pltpu.VMEM
-    piece = [(fh, 128), (128, fh), (128, fh), (vw // 2, 128), (128, (2 * qk + vw) // 2)]
+    piece = [(ffp, 128), (fh, 128), (fh, 128), (vw, 128), (128, 2 * qk + vw)]
     scratch = dict(
         lsem=dma((20,)),
         gs=[dma((ng, n)) for _ in range(9)],
         gnsem=[dma((n,)), dma((n,))],
         segsem=[dma((3,)), dma((4,))],
-        csem=[dma((4, 3)), dma((4, 4))],
-        hsem=[dma((5, 3)), dma((5, 4))],
+        psem=[dma((6,)), dma((6,))],
+        csem=[dma((1, 3)), dma((1, 4))],
+        hsem=[dma((2, 3)), dma((2, 4))],
         ysem=[dma((4, blocks)), dma((4, blocks))],
         kvsem=[dma((3,)), dma((4,))],
         dksem=[dma((3,)), dma((3,))],
@@ -1330,32 +1432,36 @@
         smsem=[dma((2, max(n, 3))), dma((2, max(n, 4)))],
         fqkv=vm((width, 2 * qk + vw), BF16),
         fo=vm((vw, width), BF16),
-        fg=vm((width, ffp), BF16),
-        fu=vm((width, ffp), BF16),
+        fg=vm((ffp, width), BF16),
+        fu=vm((ffp, width), BF16),
         fd=vm((ffp, width), BF16),
         xv=vm((rows, width), BF16),
         tv=vm((rows, width), BF16),
         gath=vm((n, 8, width // n), F32),
         gain=vm((8, width), F32),
+        gains=vm((8, width // n), F32),
+        segrow=vm((8, rows), F32),
+        segcol=vm((rows, 128), F32),
+        valid=vm((rows, 128), F32),
         segall=vm((4, 8, rows), F32),
         n1=vm((rows, width), BF16),
         n2=vm((rows, width), BF16),
         dy=vm((rows, width), BF16),
         da=vm((rows, width), BF16),
-        n1c=vm((4 * rows, half_d), BF16),
+        n1c=vm((2 * rows, half_d), BF16),
         n2c=vm((4 * rows, half_d), BF16),
-        dyc=vm((4 * rows, half_d), BF16),
-        dac=vm((4 * rows, half_d), BF16),
+        dyc=vm((2 * rows, half_d), BF16),
+        dac=vm((2 * rows, half_d), BF16),
         hid=vm((rows, ffp), BF16),
         dg=vm((rows, ffp), BF16),
         du=vm((rows, ffp), BF16),
         mix=vm((rows, vw), BF16),
         dqkv=vm((rows, 2 * qk + vw), BF16),
-        hidx=vm((4 * rows, fh), BF16),
+        hidx=vm((2 * rows, ffp), BF16),
         dgx=vm((4 * rows, fh), BF16),
         dux=vm((4 * rows, fh), BF16),
-        mixx=vm((4 * rows, vw // 2), BF16),
-        dqkvx=vm((4 * rows, (2 * qk + vw) // 2), BF16),
+        mixx=vm((2 * rows, vw), BF16),
+        dqkvx=vm((2 * rows, 2 * qk + vw), BF16),
         ysend=vm((4, blocks, rows, 256), BF16),
         yrecv=vm((4, blocks, rows, 256), BF16),
         q=vm((rows, qk), BF16),
@@ -1376,9 +1482,11 @@
         dkv=vm((rows, qk + vw), F32),
         dkvp=vm((4, rows, qk + vw), BF16),
         back=vm((3, rows, qk + vw), BF16),
-        turned=vm((max(fh, half_d), 4 * rows), BF16),
+        turned=vm((max(ffp, half_d), 4 * rows), BF16),
         part=[vm((n,) + s, BF16) for s in piece],
         seen=[vm((n + 1,) + s, BF16) for s in piece],
+        other=[vm(piece[i], BF16) for i in (0, 3, 4)],
+        out_q=vm((width // n, 2 * qk + vw), BF16),
     )
     flat, layout = [], []
     for k, v in scratch.items():
@@ -1416,38 +1524,19 @@
     )(*inputs.values())
     o = SimpleNamespace(**dict(zip(outs, res)))
 
-    def rows_of(a, total):
-        w = a.shape[2]
-        keep = total - w
-        return jnp.concatenate(
-            [jnp.concatenate([a[cc], a[2 + cc][:, w - (up_to(total, 128) - w) : w - (up_to(total, 128) - total)]], axis=1) for cc in range(2)],
-            axis=0,
-        ).astype(F32)
-
-    def cols_of(a, total):
-        w = a.shape[1]
-        return jnp.concatenate(
-            [jnp.concatenate([a[cc], a[2 + cc][w - (up_to(total, 128) - w) : w - (up_to(total, 128) - total)]], axis=0) for cc in range(2)],
-            axis=1,
-        ).astype(F32)
-
-    gq = rows_of(o.out_q, 2 * qk + vw)
-    lo = lax.axis_index("fsdp") * (width // n)
-    mine = lax.dynamic_slice_in_dim(o.sums, lo, width // n, axis=1)
-    loss = jnp.sum(o.sums[2]) / (o.sums[3, 0] * width)
     return (
         o.layer_out[None],
         o.grad_in[None],
-        mine[0],
-        gq[:, :qk],
-        gq[:, qk : 2 * qk],
-        gq[:, 2 * qk :],
-        cols_of(o.out_o, vw),
-        mine[1],
-        rows_of(o.out_g, ff),
-        rows_of(o.out_u, ff),
-        cols_of(o.out_d, ff),
-        loss,
+        o.grad_attn[0],
+        o.grad_q,
+        o.grad_k,
+        o.grad_v,
+        o.out_o.astype(F32),
+        o.grad_ffn[0],
+        o.out_g[:ff].astype(F32).T,
+        o.out_u[:ff].astype(F32).T,
+        o.out_d[:ff].astype(F32),
+        o.loss[0, 0],
     )
 
 

time: 251 us -> 214 us (0.85)
  Pallas kernels: 226 us -> 201 us
  local copies, waits for them, and re-layouts: 14.8 us -> 4.85 us
    pallas_call x1, Pallas kernels: 226 us -> 201 us  [mega(): pl.pallas_call(kernel, out_shape=[jax.ShapeDtypeStruct(*v) for v in outs....]
    transpose x0 -> x1, other arithmetic: none -> 3.15 us  [mega(): o.out_u[:ff].astype(F32)]
    slice x7 -> x0, local copies, waits for them, and re-layouts: 2.7 us -> none  [the longest x1 1.42 us: mega(): mine[1]]
    unnamed x24 -> x25, local copies, waits for them, and re-layouts: 6.45 us -> 4.85 us
where the time goes in v3:
time: 214 us
  Pallas kernels  201 us (94%)
  other arithmetic  5.17 us (2%)
  local copies, waits for them, and re-layouts  4.85 us (2%)
  between operations  2.51 us (1%)
    pallas_call x1, Pallas kernels, mega(): pl.pallas_call(kernel, out_shape=[jax.ShapeDtypeStruct(*v) for v in outs....  201 us
    unnamed x25, local copies, waits for them, and re-layouts  4.85 us

profile of v3, /device:TPU:0, one launch (start us, length us, event | category | flops | bytes accessed | tf_op | source)
XLA Modules:
  0.0 213.8 jit_solution(10919719638748641355)
XLA Ops:
  0.6 201.3 %block_step.1 = (bf16[256,1024]{1,0:T(8,128)(2,1)}, bf16[256,1024]{1,0:T(8,128)(2,1)}, bf16[1408,256]{1,0:T(8,128)(2,1)}, bf16[1408,256]{1,0:T(8,128)(2,1)}, bf1...) custom-call(bf16[256,1024]{1,0:T(8,128)(2,1)} %bitcast.17, ...), custom_call_target="tpu_custom_call" | custom-call | tf_op jit(solution)/shard_map/block_step/pallas_call | solution.py:1514
  202.0 0.0 copy-start
  202.0 3.1 %convert_bitcast_fusion = (f32[256,1376]{0,1:T(8,128)}, f32[256,1376]{0,1:T(8,128)}) fusion(bf16[1408,256]{1,0:T(8,128)(2,1)} %get-tuple-element.33, bf16[1408,256]{1,0:T(8,128)(2,1)} %get-tuple-element.32), kind=kLoop, calls=%fused_computation | loop fusion | flops 704512 | bytes 4227072 | tf_op jit(solution)/shard_map/transpose | solution.py:1537
  205.1 0.0 copy-start.4
  205.1 0.0 copy-done
  205.1 0.0 copy-start.3
  205.1 1.2 slice_convert_fusion
  206.3 0.0 copy-start.2
  206.3 0.0 copy-done.4
  206.3 0.0 copy-start.8
  206.3 0.0 copy-start.6
  206.3 0.0 copy-start.5
  206.4 0.8 convert_element_type.8
  207.2 0.0 copy-start.1
  207.2 0.0 copy-done.3
  207.2 0.8 copy.33
  208.0 0.0 copy-done.2
  208.0 0.0 copy-start.7
  208.0 0.8 copy.34
  208.8 0.0 copy-done.8
  208.8 0.6 copy.35
  209.3 0.0 copy-done.6
  209.3 0.7 copy.36
  210.0 0.0 copy-done.5
  210.0 0.7 copy.37
  210.7 0.0 copy-done.1
  210.7 0.8 copy.38
  211.5 0.0 copy-done.7
  211.5 0.6 copy.39
Async XLA Ops:
  202.0 3.2 %copy-start = (bf16[1408,256]{1,0:T(8,128)(2,1)S(1)}, bf16[1408,256]{1,0:T(8,128)(2,1)}, u32[]{:S(2)}) copy-start(bf16[1408,256]{1,0:T(8,128)(2,1)} %get-tuple-element.34) | copy-start | bytes 2162692
  205.1 1.2 copy-start.4
  205.1 2.1 copy-start.3
  206.3 1.7 copy-start.2
  206.3 2.4 %copy-start.8 = (f32[1,256]{1,0:T(1,128)S(1)}, f32[1,256]{1,0:T(1,128)}, u32[]{:S(2)}) copy-start(f32[1,256]{1,0:T(1,128)} %get-tuple-element.26) | copy-start | bytes 3076
  206.3 3.0 %copy-start.6 = (f32[256,128]{1,0:T(8,128)S(1)}, f32[256,128]{1,0:T(8,128)}, u32[]{:S(2)}) copy-start(f32[256,128]{1,0:T(8,128)} %get-tuple-element.53) | copy-start | bytes 393220
  206.3 3.7 %copy-start.5 = (f32[256,128]{1,0:T(8,128)S(1)}, f32[256,128]{1,0:T(8,128)}, u32[]{:S(2)}) copy-start(f32[256,128]{1,0:T(8,128)} %get-tuple-element.54) | copy-start | bytes 393220
  207.2 3.5 %copy-start.1 = (f32[256,512]{1,0:T(8,128)S(1)}, f32[256,512]{1,0:T(8,128)}, u32[]{:S(2)}) copy-start(f32[256,512]{1,0:T(8,128)} %get-tuple-element.55) | copy-start | bytes 1572868
  208.0 3.5 %copy-start.7 = (f32[1,256]{1,0:T(1,128)S(1)}, f32[1,256]{1,0:T(1,128)}, u32[]{:S(2)}) copy-start(f32[1,256]{1,0:T(1,128)} %get-tuple-element.31) | copy-start | bytes 3076

commit v4 on v3

--- a/solution.py
+++ b/solution.py
@@ -489,6 +489,11 @@
                 self.cross(g, s, 1 - p.x, p.c).wait_recv()
                 self.chip(g, s, 1 - p.x, p.c, True).start()
 
+    def whole(self, g, s):
+        p = self.p
+        self.chip(g, s, p.x, 1 - p.c, False).wait_recv()
+        self.chip(g, s, 1 - p.x, 1 - p.c, True).wait_recv()
+
     def finish(self, g):
         p = self.p
 
@@ -496,8 +501,7 @@
         def _(s):
             @pl.when(s != p.z)
             def _():
-                self.chip(g, s, p.x, 1 - p.c, False).wait_recv()
-                self.chip(g, s, 1 - p.x, 1 - p.c, True).wait_recv()
+                self.whole(g, s)
 
     def drain(self):
         p = self.p
@@ -593,11 +597,16 @@
 
     def mine(self, g):
         p = self.p
+        if self.done[g].shape[1] != 256:
+            return self.parts[g].at[p.z]
         half = self.done[g].shape[0] // 2
         skip = self.parts[g].shape[1] - half
         return self.parts[g].at[p.z, pl.ds(pl.multiple_of(p.x * skip, 16), half), :]
 
     def block(self, g, x, c):
+        if self.done[g].shape[1] != 256:
+            w = self.done[g].shape[1] // 2
+            return self.done[g].at[pl.ds(at128(c * 128), 128), pl.ds(at128(x * w), w)]
         half = self.done[g].shape[0] // 2
         return self.done[g].at[pl.ds(pl.multiple_of(x * half, 16), half), pl.ds(at128(c * 128), 128)]
 
@@ -606,10 +615,7 @@
         return remote(dst if src is None else src, dst, self.fs.at[g, which], self.fr.at[g, slot], ctx=to)
 
     def side(self, g, c):
-        at = pl.ds(at128(c * 128), 128)
-        if self.done[g].shape[1] == 256:
-            return self.done[g].at[:, at]
-        return self.done[g].at[at, :]
+        return self.done[g].at[:, pl.ds(at128(c * 128), 128)]
 
     def across(self, g):
         p = self.p
@@ -932,6 +938,11 @@
                 between[ch]()
 
     def y_rows(i, rs):
+        if i == 1:
+            parts = [(s, slice(cc * 128, cc * 128 + 128)) for cc in range(2) for s in range(n)]
+            return jnp.concatenate(
+                [ysend[1, s, rs, at].astype(F32) + yrecv[1, s, rs, at].astype(F32) for s, at in parts], axis=1
+            )
         return jnp.concatenate(
             [ysend[i, ch, rs, :].astype(F32) + yrecv[i, ch, rs, :].astype(F32) for ch in range(blocks)], axis=1
         )
@@ -1050,6 +1061,34 @@
 
     per_rows(norm_two)
 
+    red = Reduce(
+        p,
+        [r.part[i] for i in range(5)],
+        [r.seen[i] for i in range(5)],
+        [r.out_d, r.out_g, r.out_u, r.out_o, r.out_q],
+        [r.other, None, None, None, None],
+        r.rsem,
+    )
+    turned = r.turned
+
+    def turn(src):
+        w = src.shape[1]
+
+        @pl.loop(0, src.shape[0] // rows_here)
+        def _(i):
+            at = pl.ds(pl.multiple_of(i * rows_here, rows_here), rows_here)
+            turned[0:w, at] = jnp.transpose(src[at, :])
+
+    def grad_cols(g, rhs):
+        rows = r.part[g].shape[1]
+
+        @pl.loop(0, -(-rows // 256))
+        def _(i):
+            at = pl.ds(at128(jnp.minimum(i * 256, rows - 256)), 256)
+            res = mm(turned[at, 0 : rhs.shape[0]], rhs[...]).astype(BF16)
+            for s in range(n):
+                r.part[g][s, at, :] = res[:, s * 128 : s * 128 + 128]
+
     fchunks = -(-ffp // 256)
 
     def per_ff(body):
@@ -1072,13 +1111,32 @@
 
     per_ff(forward_ff)
     send_hid.start()
-    ready(6, ng)
-    for ch in range(blocks):
-        y_put(1, ch, mm(r.hid[...], fd[:, ch * 256 : ch * 256 + 256]))
+
+    def down_block(s):
+        for cc in range(2):
+            cols = pl.ds(at128((cc * n + s) * 128), 128)
+            ysend[1, s, :, cc * 128 : cc * 128 + 128] = mm(r.hid[...], fd[:, cols]).astype(BF16)
+        y_copy(1, s).start()
+
+    advance(ng - 1)
+    down_block(z)
+    for h in range(1, n):
+        advance(ng - 1 + 0.7 * h + 0.81)
+        for s, there in ((z + h, z + h < n), (z - h, z - h >= 0)):
+
+            @pl.when(there)
+            def _():
+                for g in range(6, ng):
+                    gather.whole(g, s)
+                down_block(s)
+
+    advance(2 * ng)
     send_n2.start()
     get_teacher.wait()
     small = r.small
     small[...] = jnp.zeros_like(small)
+    send_hid.wait()
+    turn(r.hidx)
     y_wait(1)
 
     def finish_forward(rs):
@@ -1107,54 +1165,13 @@
     per_ff(backward_ff)
     send_dg.start()
     send_du.start()
+    send_dy.wait()
+    grad_cols(0, r.dyc)
+    red.stage(0, 0)
     for ch in range(blocks):
         cols = slice(ch * 256, ch * 256 + 256)
         y_put(2, ch, mm(r.dg[...], fg[:, cols]) + mm(r.du[...], fu[:, cols]))
 
-    red = Reduce(
-        p,
-        [r.part[i] for i in range(5)],
-        [r.seen[i] for i in range(5)],
-        [r.out_d, r.out_g, r.out_u, r.out_o, r.out_q],
-        [r.other[0], None, None, r.other[1], r.other[2]],
-        r.rsem,
-    )
-    turned = r.turned
-
-    def turn(src):
-        w = src.shape[1]
-
-        @pl.loop(0, src.shape[0] // rows_here)
-        def _(i):
-            at = pl.ds(pl.multiple_of(i * rows_here, rows_here), rows_here)
-            turned[0:w, at] = jnp.transpose(src[at, :])
-
-    def grad_rows(g, rhs):
-        rows = r.part[g].shape[1]
-
-        @pl.loop(0, rhs.shape[1] // 128 // 2 if rhs.shape[1] % 256 == 0 else rhs.shape[1] // 128)
-        def _(i):
-            w = 256 if rhs.shape[1] % 256 == 0 else 128
-            at = pl.ds(at128(i * w), w)
-            res = mm(turned[0 : n * rows, 0 : rhs.shape[0]], rhs[:, at]).astype(BF16)
-            for s in range(n):
-                r.part[g][s, :, at] = res[s * rows : s * rows + rows, :]
-
-    def grad_cols(g, rhs):
-        rows = r.part[g].shape[1]
-
-        @pl.loop(0, -(-rows // 256))
-        def _(i):
-            at = pl.ds(at128(jnp.minimum(i * 256, rows - 256)), 256)
-            res = mm(turned[at, 0 : rhs.shape[0]], rhs[...]).astype(BF16)
-            for s in range(n):
-                r.part[g][s, at, :] = res[:, s * 128 : s * 128 + 128]
-
-    send_hid.wait()
-    turn(r.hidx)
-    send_dy.wait()
-    grad_cols(0, r.dyc)
-    red.stage(0, 0)
     send_dg.relay()
 
     y_wait(2)
@@ -1174,7 +1191,6 @@
 
     per_rows(middle_back)
     send_da.start()
-    send_du.relay()
     send_n2.wait()
     send_dg.wait()
     turn(r.dgx)
@@ -1187,6 +1203,36 @@
         d = mm_nt(r.da[...], fo[at, :]) * den[:, at]
         dnum[:, at] = d.astype(BF16)
         dden[:, at] = d * num[:, at]
+    send_du.relay()
+    send_da.wait()
+    send_mix.wait()
+    turn(r.mixx)
+
+    def out_half(dst, xx):
+        rows = vw // 2
+        res = mm(turned[pl.ds(pl.multiple_of(xx * rows, 128), rows), 0 : 2 * rows_here], r.dac[...]).astype(BF16)
+        for s in range(n):
+            dst[s] = res[:, s * 128 : s * 128 + 128]
+
+    def halve(i, g, make):
+        give, got = r.give[i], r.got[i]
+        make(give, 1 - x)
+        half_copy(i).start()
+        make(r.part[g], x)
+
+    def half_copy(i):
+        return remote(r.give[i], r.got[i], r.presem[0].at[i], r.presem[1].at[i], ctx=p.xp)
+
+    def joined(i, g):
+        half_copy(i).wait_recv()
+        for s in range(n):
+            r.part[g][s] = (r.part[g][s].astype(F32) + r.got[i][s].astype(F32)).astype(BF16)
+
+    halve(0, 3, out_half)
+    send_du.wait()
+    turn(r.dux)
+    grad_cols(2, r.n2c)
+    red.stage(2, 0)
     dkvp, dkv, dq = r.dkvp, r.dkv, r.dqf
     dq[...] = jnp.zeros_like(dq)
 
@@ -1220,6 +1266,7 @@
         back_block(j)
         dkvp[j] = dkv[...].astype(BF16)
 
+    red.stage(0, 1)
     dks, dkr = r.dksem
     back = r.back
 
@@ -1233,8 +1280,6 @@
     @pl.when(x == 1)
     def _():
         dk_copy(dkvp.at[1 - c], 1, 1, p.ic).start()
-
-    back_block(b)
 
     @pl.when(x == 1)
     def _():
@@ -1242,6 +1287,8 @@
         dkvp[b] = (dkvp[c].astype(F32) + back[1].astype(F32)).astype(BF16)
         dk_copy(dkvp.at[b], 2, 2, p.xp).start()
 
+    back_block(b)
+
     @pl.when(c == 0)
     def _():
         dk_copy(dkvp.at[b], 0, 0, p.ic).wait_recv()
@@ -1249,15 +1296,7 @@
 
     dqkv = r.dqkv
     dqkv[:, 0:qk] = dq[...].astype(BF16)
-    send_du.wait()
-    turn(r.dux)
-    grad_cols(2, r.n2c)
-    red.stage(2, 0)
-    red.stage(0, 1)
-    send_da.wait()
-    send_mix.wait()
-    turn(r.mixx)
-    grad_cols(3, r.dac)
+    joined(0, 3)
     red.stage(3, 0)
     red.stage(1, 1)
 
@@ -1273,9 +1312,18 @@
     send_n1.wait()
     turn(r.n1c)
     send_dqkv.wait()
-    grad_rows(4, r.dqkvx)
+
+    def qkv_half(dst, xx):
+        cols = (2 * qk + vw) // 2
+        rhs = r.dqkvx[:, pl.ds(at128(xx * cols), cols)]
+        res = mm(turned[0:half_d, 0 : 2 * rows_here], rhs).astype(BF16)
+        for s in range(n):
+            dst[s] = res[s * 128 : s * 128 + 128, :]
+
+    halve(1, 4, qkv_half)
+    red.stage(0, 2)
+    joined(1, 4)
     red.stage(4, 0)
-    red.stage(0, 2)
     red.stage(2, 1)
     red.last(0)
 
@@ -1339,6 +1387,8 @@
             r.grad_k[...] = r.out_q[:, qk : 2 * qk].astype(F32)
             r.grad_v[...] = r.out_q[:, 2 * qk : 2 * qk + vw].astype(F32)
 
+    for i in range(2):
+        half_copy(i).wait_send()
     gather.drain()
     for k in (send_n1, send_da, send_n2, send_dy, send_hid, send_dg, send_du, send_mix, send_dqkv):
         k.drain()
@@ -1416,7 +1466,7 @@
     dma = pltpu.SemaphoreType.DMA
     ng = 8
     vm = pltpu.VMEM
-    piece = [(ffp, 128), (fh, 128), (fh, 128), (vw, 128), (128, 2 * qk + vw)]
+    piece = [(ffp, 128), (fh, 128), (fh, 128), (vw // 2, 128), (128, (2 * qk + vw) // 2)]
     scratch = dict(
         lsem=dma((20,)),
         gs=[dma((ng, n)) for _ in range(9)],
@@ -1462,7 +1512,7 @@
         dux=vm((4 * rows, fh), BF16),
         mixx=vm((2 * rows, vw), BF16),
         dqkvx=vm((2 * rows, 2 * qk + vw), BF16),
-        ysend=vm((4, blocks, rows, 256), BF16),
+        ysend=vm((4, max(blocks, n), rows, 256), BF16),
         yrecv=vm((4, blocks, rows, 256), BF16),
         q=vm((rows, qk), BF16),
         kv=vm((4, rows, qk + vw), BF16),
@@ -1485,7 +1535,10 @@
         turned=vm((max(ffp, half_d), 4 * rows), BF16),
         part=[vm((n,) + s, BF16) for s in piece],
         seen=[vm((n + 1,) + s, BF16) for s in piece],
-        other=[vm(piece[i], BF16) for i in (0, 3, 4)],
+        other=vm(piece[0], BF16),
+        give=[vm((n,) + piece[i], BF16) for i in (3, 4)],
+        got=[vm((n,) + piece[i], BF16) for i in (3, 4)],
+        presem=[dma((2,)), dma((2,))],
         out_q=vm((width // n, 2 * qk + vw), BF16),
     )
     flat, layout = [], []

time: 214 us -> 193 us (0.902)
  Pallas kernels: 201 us -> 180 us
    pallas_call x1, Pallas kernels: 201 us -> 180 us  [mega(): pl.pallas_call(kernel, out_shape=[jax.ShapeDtypeStruct(*v) for v in outs....]
where the time goes in v4:
time: 193 us
  Pallas kernels  180 us (93%)
  other arithmetic  5.17 us (3%)
  local copies, waits for them, and re-layouts  4.85 us (3%)
  between operations  2.51 us (1%)
    pallas_call x1, Pallas kernels, mega(): pl.pallas_call(kernel, out_shape=[jax.ShapeDtypeStruct(*v) for v in outs....  180 us
    unnamed x25, local copies, waits for them, and re-layouts  4.85 us

profile of v4, /device:TPU:0, one launch (start us, length us, event | category | flops | bytes accessed | tf_op | source)
XLA Modules:
  0.0 192.7 jit_solution(11542480624095201239)
XLA Ops:
  0.6 180.2 %block_step.1 = (bf16[256,1024]{1,0:T(8,128)(2,1)}, bf16[256,1024]{1,0:T(8,128)(2,1)}, bf16[1408,256]{1,0:T(8,128)(2,1)}, bf16[1408,256]{1,0:T(8,128)(2,1)}, bf1...) custom-call(bf16[256,1024]{1,0:T(8,128)(2,1)} %bitcast.17, ...), custom_call_target="tpu_custom_call" | custom-call | tf_op jit(solution)/shard_map/block_step/pallas_call | solution.py:1567
  180.9 0.0 copy-start
  180.9 3.1 %convert_bitcast_fusion = (f32[256,1376]{0,1:T(8,128)}, f32[256,1376]{0,1:T(8,128)}) fusion(bf16[1408,256]{1,0:T(8,128)(2,1)} %get-tuple-element.33, bf16[1408,256]{1,0:T(8,128)(2,1)} %get-tuple-element.32), kind=kLoop, calls=%fused_computation | loop fusion | flops 704512 | bytes 4227072 | tf_op jit(solution)/shard_map/transpose | solution.py:1590
  184.0 0.0 copy-start.4
  184.0 0.0 copy-done
  184.0 0.0 copy-start.3
  184.0 1.2 slice_convert_fusion
  185.2 0.0 copy-start.2
  185.2 0.0 copy-done.4
  185.2 0.0 copy-start.8
  185.2 0.0 copy-start.6
  185.2 0.0 copy-start.5
  185.2 0.8 convert_element_type.8
  186.1 0.0 copy-start.1
  186.1 0.0 copy-done.3
  186.1 0.8 copy.33
  186.9 0.0 copy-done.2
  186.9 0.0 copy-start.7
  186.9 0.8 copy.34
  187.7 0.0 copy-done.8
  187.7 0.6 copy.35
  188.2 0.0 copy-done.6
  188.2 0.7 copy.36
  188.9 0.0 copy-done.5
  188.9 0.7 copy.37
  189.5 0.0 copy-done.1
  189.5 0.8 copy.38
  190.3 0.0 copy-done.7
  190.3 0.6 copy.39
Async XLA Ops:
  180.9 3.2 %copy-start = (bf16[1408,256]{1,0:T(8,128)(2,1)S(1)}, bf16[1408,256]{1,0:T(8,128)(2,1)}, u32[]{:S(2)}) copy-start(bf16[1408,256]{1,0:T(8,128)(2,1)} %get-tuple-element.34) | copy-start | bytes 2162692
  184.0 1.2 copy-start.4
  184.0 2.1 %copy-start.3 = (bf16[256,1024]{1,0:T(8,128)(2,1)S(1)}, bf16[256,1024]{1,0:T(8,128)(2,1)}, u32[]{:S(2)}) copy-start(bf16[256,1024]{1,0:T(8,128)(2,1)} %get-tuple-element.24) | copy-start | bytes 1572868
  185.2 1.7 copy-start.2
  185.2 2.4 %copy-start.8 = (f32[1,256]{1,0:T(1,128)S(1)}, f32[1,256]{1,0:T(1,128)}, u32[]{:S(2)}) copy-start(f32[1,256]{1,0:T(1,128)} %get-tuple-element.26) | copy-start | bytes 3076
  185.2 3.0 %copy-start.6 = (f32[256,128]{1,0:T(8,128)S(1)}, f32[256,128]{1,0:T(8,128)}, u32[]{:S(2)}) copy-start(f32[256,128]{1,0:T(8,128)} %get-tuple-element.53) | copy-start | bytes 393220
  185.2 3.7 %copy-start.5 = (f32[256,128]{1,0:T(8,128)S(1)}, f32[256,128]{1,0:T(8,128)}, u32[]{:S(2)}) copy-start(f32[256,128]{1,0:T(8,128)} %get-tuple-element.54) | copy-start | bytes 393220
  186.1 3.5 %copy-start.1 = (f32[256,512]{1,0:T(8,128)S(1)}, f32[256,512]{1,0:T(8,128)}, u32[]{:S(2)}) copy-start(f32[256,512]{1,0:T(8,128)} %get-tuple-element.55) | copy-start | bytes 1572868
  186.9 3.5 %copy-start.7 = (f32[1,256]{1,0:T(1,128)S(1)}, f32[1,256]{1,0:T(1,128)}, u32[]{:S(2)}) copy-start(f32[1,256]{1,0:T(1,128)} %get-tuple-element.31) | copy-start | bytes 3076

commit v5 on v4

--- a/solution.py
+++ b/solution.py
@@ -888,11 +888,11 @@
             [gath[s, row : row + 1, cc * 128 : cc * 128 + 128] for cc in range(2) for s in range(n)], axis=1
         )
 
-    events = [(g - 1.5, "own", g, 0) for g in range(2, ng)]
+    events = [(g - 0.7, "own", g, 0) for g in range(2, ng)]
     for g in range(ng):
         for h in range(1, n):
-            events.append((g + 0.7 * h, "hop", g, h))
-            events.append((g + 0.7 * h + 0.8, "cross", g, h))
+            events.append((g + 0.6 * h, "hop", g, h))
+            events.append((g + 0.6 * h + 0.8, "cross", g, h))
     events.sort()
     passed = [0]
 
@@ -1037,9 +1037,13 @@
     def _():
         kv_copy(1 - c, 2, p.ic).wait_recv()
 
-    @pl.loop(1, b + 1)
-    def _(m):
-        attend_block(b - m)
+    for m in range(1, 4):
+
+        @pl.when(b >= m)
+        def _():
+            attend_block(b - m)
+
+        advance(3.3 + 0.3 * m)
 
     inv = 1.0 / den[...]
     den[...] = inv
@@ -1121,7 +1125,7 @@
     advance(ng - 1)
     down_block(z)
     for h in range(1, n):
-        advance(ng - 1 + 0.7 * h + 0.81)
+        advance(ng - 1 + 0.6 * h + 0.81)
         for s, there in ((z + h, z + h < n), (z - h, z - h >= 0)):
 
             @pl.when(there)

time: 193 us -> 188 us (0.974)
  Pallas kernels: 180 us -> 175 us
    pallas_call x1, Pallas kernels: 180 us -> 175 us  [mega(): pl.pallas_call(kernel, out_shape=[jax.ShapeDtypeStruct(*v) for v in outs....]
where the time goes in v5:
time: 188 us
  Pallas kernels  175 us (93%)
  other arithmetic  5.17 us (3%)
  local copies, waits for them, and re-layouts  4.85 us (3%)
  between operations  2.51 us (1%)
    pallas_call x1, Pallas kernels, mega(): pl.pallas_call(kernel, out_shape=[jax.ShapeDtypeStruct(*v) for v in outs....  175 us
    unnamed x25, local copies, waits for them, and re-layouts  4.85 us

profile of v5, /device:TPU:0, one launch (start us, length us, event | category | flops | bytes accessed | tf_op | source)
XLA Modules:
  0.0 187.9 jit_solution(18152546213878765187)
XLA Ops:
  0.6 175.3 %block_step.1 = (bf16[256,1024]{1,0:T(8,128)(2,1)}, bf16[256,1024]{1,0:T(8,128)(2,1)}, bf16[1408,256]{1,0:T(8,128)(2,1)}, bf16[1408,256]{1,0:T(8,128)(2,1)}, bf1...) custom-call(bf16[256,1024]{1,0:T(8,128)(2,1)} %bitcast.17, ...), custom_call_target="tpu_custom_call" | custom-call | tf_op jit(solution)/shard_map/block_step/pallas_call | solution.py:1571
  176.0 0.0 copy-start
  176.0 3.1 %convert_bitcast_fusion = (f32[256,1376]{0,1:T(8,128)}, f32[256,1376]{0,1:T(8,128)}) fusion(bf16[1408,256]{1,0:T(8,128)(2,1)} %get-tuple-element.33, bf16[1408,256]{1,0:T(8,128)(2,1)} %get-tuple-element.32), kind=kLoop, calls=%fused_computation | loop fusion | flops 704512 | bytes 4227072 | tf_op jit(solution)/shard_map/transpose | solution.py:1594
  179.2 0.0 copy-start.4
  179.2 0.0 copy-done
  179.2 0.0 copy-start.3
  179.2 1.2 slice_convert_fusion
  180.4 0.0 copy-start.2
  180.4 0.0 copy-done.4
  180.4 0.0 copy-start.8
  180.4 0.0 copy-start.6
  180.4 0.0 copy-start.5
  180.4 0.8 convert_element_type.8
  181.2 0.0 copy-start.1
  181.2 0.0 copy-done.3
  181.2 0.8 copy.33
  182.0 0.0 copy-done.2
  182.0 0.0 copy-start.7
  182.0 0.8 copy.34
  182.8 0.0 copy-done.8
  182.8 0.6 copy.35
  183.4 0.0 copy-done.6
  183.4 0.7 copy.36
  184.0 0.0 copy-done.5
  184.0 0.7 copy.37
  184.7 0.0 copy-done.1
  184.7 0.8 copy.38
  185.5 0.0 copy-done.7
  185.5 0.6 copy.39
Async XLA Ops:
  176.0 3.2 %copy-start = (bf16[1408,256]{1,0:T(8,128)(2,1)S(1)}, bf16[1408,256]{1,0:T(8,128)(2,1)}, u32[]{:S(2)}) copy-start(bf16[1408,256]{1,0:T(8,128)(2,1)} %get-tuple-element.34) | copy-start | bytes 2162692
  179.2 1.2 copy-start.4
  179.2 2.1 %copy-start.3 = (bf16[256,1024]{1,0:T(8,128)(2,1)S(1)}, bf16[256,1024]{1,0:T(8,128)(2,1)}, u32[]{:S(2)}) copy-start(bf16[256,1024]{1,0:T(8,128)(2,1)} %get-tuple-element.24) | copy-start | bytes 1572868
  180.4 1.7 copy-start.2
  180.4 2.4 %copy-start.8 = (f32[1,256]{1,0:T(1,128)S(1)}, f32[1,256]{1,0:T(1,128)}, u32[]{:S(2)}) copy-start(f32[1,256]{1,0:T(1,128)} %get-tuple-element.26) | copy-start | bytes 3076
  180.4 3.0 %copy-start.6 = (f32[256,128]{1,0:T(8,128)S(1)}, f32[256,128]{1,0:T(8,128)}, u32[]{:S(2)}) copy-start(f32[256,128]{1,0:T(8,128)} %get-tuple-element.53) | copy-start | bytes 393220
  180.4 3.7 %copy-start.5 = (f32[256,128]{1,0:T(8,128)S(1)}, f32[256,128]{1,0:T(8,128)}, u32[]{:S(2)}) copy-start(f32[256,128]{1,0:T(8,128)} %get-tuple-element.54) | copy-start | bytes 393220
  181.2 3.5 %copy-start.1 = (f32[256,512]{1,0:T(8,128)S(1)}, f32[256,512]{1,0:T(8,128)}, u32[]{:S(2)}) copy-start(f32[256,512]{1,0:T(8,128)} %get-tuple-element.55) | copy-start | bytes 1572868
  182.0 3.5 %copy-start.7 = (f32[1,256]{1,0:T(1,128)S(1)}, f32[1,256]{1,0:T(1,128)}, u32[]{:S(2)}) copy-start(f32[1,256]{1,0:T(1,128)} %get-tuple-element.31) | copy-start | bytes 3076

commit v6 on v5

--- a/solution.py
+++ b/solution.py
@@ -1233,10 +1233,6 @@
             r.part[g][s] = (r.part[g][s].astype(F32) + r.got[i][s].astype(F32)).astype(BF16)
 
     halve(0, 3, out_half)
-    send_du.wait()
-    turn(r.dux)
-    grad_cols(2, r.n2c)
-    red.stage(2, 0)
     dkvp, dkv, dq = r.dkvp, r.dkv, r.dqf
     dq[...] = jnp.zeros_like(dq)
 
@@ -1291,6 +1287,10 @@
         dkvp[b] = (dkvp[c].astype(F32) + back[1].astype(F32)).astype(BF16)
         dk_copy(dkvp.at[b], 2, 2, p.xp).start()
 
+    send_du.wait()
+    turn(r.dux)
+    grad_cols(2, r.n2c)
+    red.stage(2, 0)
     back_block(b)
 
     @pl.when(c == 0)
@@ -1366,6 +1366,9 @@
     red.stage(4, 2)
     red.relay(1)
     red.last(4)
+    red.relay(2)
+    red.relay(3)
+    red.relay(4)
     for s in range(n):
 
         @pl.when(z != s)
@@ -1381,9 +1384,6 @@
         r.grad_attn[0:1, cc * 128 : cc * 128 + 128] = r.gain[0:1, at]
         r.grad_ffn[0:1, cc * 128 : cc * 128 + 128] = r.gain[1:2, at]
     r.loss[...] = jnp.sum(total[2:3, :], axis=1, keepdims=True) / (total[3:4, 0:1] * width)
-    red.relay(2)
-    red.relay(3)
-    red.relay(4)
     for g in (4, 0, 1, 2, 3):
         red.finish(g)
         if g == 4:

time: 188 us -> 186 us (0.989)
  Pallas kernels: 175 us -> 173 us
    pallas_call x1, Pallas kernels: 175 us -> 173 us  [mega(): pl.pallas_call(kernel, out_shape=[jax.ShapeDtypeStruct(*v) for v in outs....]
where the time goes in v6:
time: 186 us; the launch traced here: 185 us
  Pallas kernels  173 us (93%)
  other arithmetic  5.17 us (3%)
  local copies, waits for them, and re-layouts  4.85 us (3%)
  between operations  2.51 us (1%)
    pallas_call x1, Pallas kernels, mega(): pl.pallas_call(kernel, out_shape=[jax.ShapeDtypeStruct(*v) for v in outs....  173 us
    unnamed x25, local copies, waits for them, and re-layouts  4.85 us

profile of v6, /device:TPU:0, one launch (start us, length us, event | category | flops | bytes accessed | tf_op | source)
XLA Modules:
  0.0 185.1 jit_solution(3953214535470894197)
XLA Ops:
  0.6 172.6 %block_step.1 = (bf16[256,1024]{1,0:T(8,128)(2,1)}, bf16[256,1024]{1,0:T(8,128)(2,1)}, bf16[1408,256]{1,0:T(8,128)(2,1)}, bf16[1408,256]{1,0:T(8,128)(2,1)}, bf1...) custom-call(bf16[256,1024]{1,0:T(8,128)(2,1)} %bitcast.17, ...), custom_call_target="tpu_custom_call" | custom-call | tf_op jit(solution)/shard_map/block_step/pallas_call | solution.py:1571
  173.2 0.0 copy-start
  173.3 3.1 %convert_bitcast_fusion = (f32[256,1376]{0,1:T(8,128)}, f32[256,1376]{0,1:T(8,128)}) fusion(bf16[1408,256]{1,0:T(8,128)(2,1)} %get-tuple-element.33, bf16[1408,256]{1,0:T(8,128)(2,1)} %get-tuple-element.32), kind=kLoop, calls=%fused_computation | loop fusion | flops 704512 | bytes 4227072 | tf_op jit(solution)/shard_map/transpose | solution.py:1594
  176.4 0.0 copy-start.4
  176.4 0.0 copy-done
  176.4 0.0 copy-start.3
  176.4 1.2 slice_convert_fusion
  177.6 0.0 copy-start.2
  177.6 0.0 copy-done.4
  177.6 0.0 copy-start.8
  177.6 0.0 copy-start.6
  177.6 0.0 copy-start.5
  177.6 0.8 convert_element_type.8
  178.5 0.0 copy-start.1
  178.5 0.0 copy-done.3
  178.5 0.8 copy.33
  179.3 0.0 copy-done.2
  179.3 0.0 copy-start.7
  179.3 0.8 copy.34
  180.1 0.0 copy-done.8
  180.1 0.6 copy.35
  180.6 0.0 copy-done.6
  180.6 0.7 copy.36
  181.3 0.0 copy-done.5
  181.3 0.7 copy.37
  181.9 0.0 copy-done.1
  181.9 0.8 copy.38
  182.7 0.0 copy-done.7
  182.7 0.6 copy.39
Async XLA Ops:
  173.2 3.2 %copy-start = (bf16[1408,256]{1,0:T(8,128)(2,1)S(1)}, bf16[1408,256]{1,0:T(8,128)(2,1)}, u32[]{:S(2)}) copy-start(bf16[1408,256]{1,0:T(8,128)(2,1)} %get-tuple-element.34) | copy-start | bytes 2162692
  176.4 1.2 copy-start.4
  176.4 2.1 %copy-start.3 = (bf16[256,1024]{1,0:T(8,128)(2,1)S(1)}, bf16[256,1024]{1,0:T(8,128)(2,1)}, u32[]{:S(2)}) copy-start(bf16[256,1024]{1,0:T(8,128)(2,1)} %get-tuple-element.24) | copy-start | bytes 1572868
  177.6 1.7 copy-start.2
  177.6 2.4 %copy-start.8 = (f32[1,256]{1,0:T(1,128)S(1)}, f32[1,256]{1,0:T(1,128)}, u32[]{:S(2)}) copy-start(f32[1,256]{1,0:T(1,128)} %get-tuple-element.26) | copy-start | bytes 3076
  177.6 3.0 %copy-start.6 = (f32[256,128]{1,0:T(8,128)S(1)}, f32[256,128]{1,0:T(8,128)}, u32[]{:S(2)}) copy-start(f32[256,128]{1,0:T(8,128)} %get-tuple-element.53) | copy-start | bytes 393220
  177.6 3.7 %copy-start.5 = (f32[256,128]{1,0:T(8,128)S(1)}, f32[256,128]{1,0:T(8,128)}, u32[]{:S(2)}) copy-start(f32[256,128]{1,0:T(8,128)} %get-tuple-element.54) | copy-start | bytes 393220
  178.5 3.5 %copy-start.1 = (f32[256,512]{1,0:T(8,128)S(1)}, f32[256,512]{1,0:T(8,128)}, u32[]{:S(2)}) copy-start(f32[256,512]{1,0:T(8,128)} %get-tuple-element.55) | copy-start | bytes 1572868
  179.3 3.5 %copy-start.7 = (f32[1,256]{1,0:T(1,128)S(1)}, f32[1,256]{1,0:T(1,128)}, u32[]{:S(2)}) copy-start(f32[1,256]{1,0:T(1,128)} %get-tuple-element.31) | copy-start | bytes 3076
